TPU v7x, 128 devices: a whole 4x4x4 slice. The times are simulated.
128 devices in a mesh: gx: 8 (over y, core), gy: 4 (over z), gz: 4 (over x).
Axes of the slice: x: 4, y: 4, z: 4, core: 2. Of those that a mesh axis runs over, the one named last changes fastest.
Arguments:
- kappa_sq: float32 [128, 64, 512], P('gx', 'gz', 'gy'), may hold values from 0.004 to 0.4
- probe_bits: int32 [4, 128, 64, 512], P(None, 'gx', 'gz', 'gy'), may hold values from 0 to 1
Outputs:
- solution: float32 [4, 128, 64, 512], P(None, 'gx', 'gz', 'gy')
- relative_residual: float32 [4], replicated
All inputs are finite; a program needn't handle non-finite values.
Results may differ from a plain program's by a relative error of at most 0.0001.
Values sent between devices are 32-bit elements; how exact they have to be, the bound alone decides.
A program may use at most 128 MiB of HBM per device.

v0:
```python
import jax
import jax.numpy as jnp
from jax import lax
from jax.sharding import Mesh
from jax.sharding import PartitionSpec as P

LEVELS = 3
COARSE_SWEEPS = 8
ITERS = 2
GX_GY_GZ = ("gx_0", "gx_1", "gy", "gz")
GX = ("gx_0", "gx_1")


damping = 0.8


def extended(block, sides, width):
    for axis, dim in sides:
        count = lax.axis_size(axis)
        forward = [(i, i + 1) for i in range(count - 1)]
        backward = [(target, source) for source, target in forward]
        low = lax.ppermute(
            lax.slice_in_dim(block, block.shape[dim] - width, None, axis=dim), axis, forward
        )
        high = lax.ppermute(lax.slice_in_dim(block, 0, width, axis=dim), axis, backward)
        block = jnp.concatenate([low, block, high], axis=dim)
    return block


def extended_2(value, sides, width):
    edges = {}
    for axis, dim in sides:
        size, length = (lax.axis_size(axis), value.shape[dim])
        up = [(i, (i + 1) % size) for i in range(size - 1)]
        last = lax.slice_in_dim(value, length - width, length, axis=dim)
        first = lax.slice_in_dim(value, 0, width, axis=dim)
        edges[dim] = (
            lax.ppermute(last, axis, up),
            lax.ppermute(first, axis, [(b, a) for a, b in up]),
        )
    done = []
    for _, dim in sides:
        low, high = edges[dim]
        around = [(width, width) if d in done else (0, 0) for d in range(value.ndim)]
        value = jnp.concatenate([jnp.pad(low, around), value, jnp.pad(high, around)], axis=dim)
        done.append(dim)
    return value


def over_axes(value, axes):
    for axis in axes:
        value = lax.psum(value, axis)
    return value


def neighbours(padded):
    along_first = padded[..., 2:, 1:-1, 1:-1] + padded[..., :-2, 1:-1, 1:-1]
    along_second = padded[..., 1:-1, 2:, 1:-1] + padded[..., 1:-1, :-2, 1:-1]
    along_third = padded[..., 1:-1, 1:-1, 2:] + padded[..., 1:-1, 1:-1, :-2]
    return along_first + along_second + along_third


def coarsen(field):
    leading = field.shape[:-3]
    cells_first, cells_second, cells_third = field.shape[-3:]
    grouped = field.reshape(
        leading + (cells_first // 2, 2, cells_second // 2, 2, cells_third // 2, 2)
    )
    return jnp.mean(grouped, axis=(-5, -3, -1))


def refine(field):
    leading = field.shape[:-3]
    cells_first, cells_second, cells_third = field.shape[-3:]
    spread = field.reshape(leading + (cells_first, 1, cells_second, 1, cells_third, 1))
    spread = jnp.broadcast_to(spread, leading + (cells_first, 2, cells_second, 2, cells_third, 2))
    return spread.reshape(leading + (cells_first * 2, cells_second * 2, cells_third * 2))


def level_faces(field, grid_level):
    if grid_level == 0:
        return extended(field, ((GX, 1), ("gy", 3), ("gz", 2)), 1)
    return extended_2(field, ((GX, 1), ("gy", 3), ("gz", 2)), 1)


def operate(field, diagonal, coupling, grid_level):
    return diagonal * field - coupling * neighbours(level_faces(field, grid_level))


def jacobi_sweep(field, rhs_field, diagonal, coupling, grid_level):
    return field + damping * (rhs_field - operate(field, diagonal, coupling, grid_level)) / diagonal


def assemble(gathered):
    count_x = lax.axis_size(GX)
    count_y = lax.axis_size("gy")
    count_z = lax.axis_size("gz")
    leading = gathered.shape[1:-3]
    cells_first, cells_second, cells_third = gathered.shape[-3:]
    lead_count = len(leading)
    blocks = gathered.reshape(
        (count_x, count_y, count_z) + leading + (cells_first, cells_second, cells_third)
    )
    permutation = tuple(range(3, 3 + lead_count)) + (
        0,
        3 + lead_count,
        2,
        4 + lead_count,
        1,
        5 + lead_count,
    )
    blocks = jnp.transpose(blocks, permutation)
    return blocks.reshape(
        leading + (count_x * cells_first, count_z * cells_second, count_y * cells_third)
    )


def local_dot(first_field, second_field):
    return jnp.sum(first_field * second_field, axis=(1, 2, 3))


def expand(values):
    return values[:, None, None, None]


def per_device(kappa_sq, probe_bits):
    diagonals = []
    couplings = []
    coef_field = kappa_sq
    for grid_level in range(LEVELS + 1):
        if grid_level > 0:
            coef_field = coarsen(coef_field)
        coupling = 0.25**grid_level
        diagonals.append(coef_field + 6.0 * coupling)
        couplings.append(coupling)
    global_diag = assemble(lax.all_gather(diagonals[LEVELS][None], GX_GY_GZ, axis=0, tiled=True))

    def coarsest(rhs_field):
        diagonal = diagonals[LEVELS]
        coupling = couplings[LEVELS]
        global_rhs = assemble(lax.all_gather(rhs_field[None], GX_GY_GZ, axis=0, tiled=True))
        field = damping * global_rhs / global_diag
        for sweep_index in range(COARSE_SWEEPS - 1):
            padded = jnp.pad(field, ((0, 0), (1, 1), (1, 1), (1, 1)))
            field = (
                field
                + damping
                * (global_rhs - (global_diag * field - coupling * neighbours(padded)))
                / global_diag
            )
        probes, block_x, block_z, block_y = rhs_field.shape
        zero_index = jnp.zeros((), jnp.int32)
        starts = (
            zero_index,
            lax.axis_index(GX) * block_x,
            lax.axis_index("gz") * block_z,
            lax.axis_index("gy") * block_y,
        )
        return lax.dynamic_slice(field, starts, (probes, block_x, block_z, block_y))

    def vcycle(rhs_field, grid_level):
        if grid_level == LEVELS:
            return coarsest(rhs_field)
        diagonal = diagonals[grid_level]
        coupling = couplings[grid_level]
        field = damping * rhs_field / diagonal
        field = jacobi_sweep(field, rhs_field, diagonal, coupling, grid_level)
        remainder = rhs_field - operate(field, diagonal, coupling, grid_level)
        field = field + refine(vcycle(coarsen(remainder), grid_level + 1))
        field = jacobi_sweep(field, rhs_field, diagonal, coupling, grid_level)
        return jacobi_sweep(field, rhs_field, diagonal, coupling, grid_level)

    right_side = 2.0 * probe_bits.astype(jnp.float32) - 1.0
    solution = jnp.zeros_like(right_side)
    residual = right_side
    fine_diag = diagonals[0]

    def pair_sums(residual_now, precond_now, operated_now):
        return (
            over_axes(local_dot(residual_now, precond_now), GX_GY_GZ),
            over_axes(local_dot(precond_now, operated_now), GX_GY_GZ),
        )

    precond = vcycle(residual, 0)
    operated = operate(precond, fine_diag, 1.0, 0)
    precond_dot, curve_dot = pair_sums(residual, precond, operated)
    step_size = precond_dot / curve_dot
    search = precond
    along = operated
    for iteration in range(ITERS):
        solution = solution + expand(step_size) * search
        residual = residual - expand(step_size) * along
        if iteration + 1 < ITERS:
            precond = vcycle(residual, 0)
            operated = operate(precond, fine_diag, 1.0, 0)
            next_dot, curve_dot = pair_sums(residual, precond, operated)
            ratio_next = next_dot / precond_dot
            step_size = next_dot / (curve_dot - ratio_next * next_dot / step_size)
            search = precond + expand(ratio_next) * search
            along = operated + expand(ratio_next) * along
            precond_dot = next_dot
    squares = lax.psum(local_dot(residual, residual), GX_GY_GZ)
    cell_total = (
        probe_bits.shape[1]
        * probe_bits.shape[2]
        * probe_bits.shape[3]
        * lax.axis_size(GX)
        * lax.axis_size("gy")
        * lax.axis_size("gz")
    )
    return (solution, jnp.sqrt(squares / cell_total))


def solution(mesh):
    finer = Mesh(
        mesh.devices.reshape(4, 2, mesh.shape["gy"], mesh.shape["gz"]), ("gx_0", "gx_1", "gy", "gz")
    )
    placed = (P(GX, "gz", "gy"), P(None, GX, "gz", "gy"))
    return jax.shard_map(
        per_device,
        mesh=finer,
        in_specs=placed,
        out_specs=(P(None, GX, "gz", "gy"), P()),
        check_vma=False,
    )
```

profile of v0, /device:TPU:0, one launch (start us, length us, event | category | flops | bytes accessed | tf_op | source)
XLA Modules:
  0.0 1091.7 jit_solution(3623767073840948052)
XLA Ops:
  11.6 4.5 collective-permute-start.2
  24.4 4.6 collective-permute-done.4
  33.4 9.7 reshape.124
  66.2 4.6 collective-permute-done.10
  71.7 8.8 copy.2403
  80.5 13.1 %reduce_sum.126 = f32[4,8,8,64]{0,3,2,1:T(8,128)} reduce(f32[4,8,2,8,2,64,2]{0,6,5,4,3,2,1:T(2,128)} %bitcast.21, f32[]{:T(128)} %constant.28.clone.1), dimensions={2,4,6}, to_apply=%region_0.0 | reduce | flops 114688 | bytes 589828 | tf_op jit(solution)/shard_map/reduce_sum | solution.py:69
  102.0 4.7 collective-permute-start.17
  114.3 4.5 collective-permute-start.19
  121.4 4.5 collective-permute-start.23
  127.3 65.5 %all-gather.1 = f32[256,2,16]{2,1,0:T(2,128)S(1)} all-gather(f32[2,2,16]{2,1,0:T(2,128)S(1)} %multiply_add_fusion.2), channel_id=3, replica_groups=mesh['gx_0'=4,'gx_1'=2,'gy'=4,'gz'=4] {'gx_0','gx_1','gy','gz'}, dimensions={0}, use_global_device_ids=true | all-gather | bytes 33024 | tf_op jit(solution)/shard_map/all_gather | solution.py:136
  207.2 4.5 collective-permute-start.29
  213.1 4.7 collective-permute-done.27
  227.2 4.5 collective-permute-start.35
  243.4 62.5 %all-gather = f32[512,2,2,16]{3,2,1,0:T(2,128)S(1)} all-gather(f32[4,2,2,16]{3,2,1,0:T(2,128)S(1)} %copy.2408), channel_id=2, replica_groups=mesh['gx_0'=4,'gx_1'=2,'gy'=4,'gz'=4] {'gx_0','gx_1','gy','gz'}, dimensions={0}, use_global_device_ids=true | all-gather | bytes 132096 | tf_op jit(solution)/shard_map/all_gather | solution.py:141
  312.8 4.5 collective-permute-start.41
  331.5 4.5 collective-permute-start.47
  337.3 4.5 collective-permute-done.45
  358.0 4.5 collective-permute-start.53
  363.9 5.6 collective-permute-done.51
  376.3 4.6 collective-permute-start.55
  383.5 4.5 collective-permute-start.59
  389.4 5.7 collective-permute-done.57
  404.0 9.0 broadcast_in_dim.14
  413.0 10.0 copy.2416
  423.1 4.6 collective-permute-start.61
  429.0 5.6 collective-permute-done.60
  437.1 5.0 collective-permute-start.62
  449.1 4.5 collective-permute-done.64
  464.6 4.5 collective-permute-start.68
  492.0 5.0 collective-permute-start.74
  509.0 11.3 %all-reduce.83 = (f32[4]{0:T(128)S(1)}, f32[4]{0:T(128)S(1)}) all-reduce(f32[4]{0:T(128)S(1)} %get-tuple-element.17, f32[4]{0:T(128)S(1)} %get-tuple-element.16), channel_id=1, replica_groups=mesh['gx_0'=4,'gx_1'=2,'gy'=4,'gz'=4] {'gx_0'}, use_global_device_ids=true, to_apply=%region_7.8 | all-reduce | flops 8 | bytes 64 | tf_op jit(solution)/shard_map/psum | solution.py:52
  522.7 12.6 %all-reduce.81 = (f32[4]{0:T(128)S(1)}, f32[4]{0:T(128)S(1)}) all-reduce(f32[4]{0:T(128)S(1)} %get-tuple-element.32, f32[4]{0:T(128)S(1)} %get-tuple-element.33), channel_id=1, replica_groups=mesh['gx_0'=4,'gx_1'=2,'gy'=4,'gz'=4] {'gy'}, use_global_device_ids=true, to_apply=%region_9.10 | all-reduce | flops 8 | bytes 64 | tf_op jit(solution)/shard_map/psum | solution.py:52
  535.3 7.7 all-reduce.79
  552.1 4.5 collective-permute-start.80
  567.3 4.6 collective-permute-done.82
  582.1 5.0 collective-permute-start.86
  600.0 8.8 copy.2467
  608.8 13.1 %reduce_sum.134 = f32[4,8,8,64]{0,3,2,1:T(8,128)} reduce(f32[4,8,2,8,2,64,2]{0,6,5,4,3,2,1:T(2,128)} %bitcast.23, f32[]{:T(128)} %constant.28.clone.1), dimensions={2,4,6}, to_apply=%region_16.17 | reduce | flops 114688 | bytes 589828 | tf_op jit(solution)/shard_map/reduce_sum | solution.py:69
  629.1 4.7 collective-permute-start.95
  635.2 5.9 collective-permute-done.93
  654.4 4.5 collective-permute-start.101
  660.3 5.9 collective-permute-done.99
  684.2 4.5 collective-permute-start.107
  706.7 4.5 collective-permute-start.113
  722.6 63.7 %all-gather.2 = f32[512,2,2,16]{3,2,1,0:T(2,128)S(1)} all-gather(f32[4,2,2,16]{3,2,1,0:T(2,128)S(1)} %copy.2472), channel_id=4, replica_groups=mesh['gx_0'=4,'gx_1'=2,'gy'=4,'gz'=4] {'gx_0','gx_1','gy','gz'}, dimensions={0}, use_global_device_ids=true | all-gather | bytes 132096 | tf_op jit(solution)/shard_map/all_gather | solution.py:141
  795.5 4.5 collective-permute-start.119
  814.3 4.5 collective-permute-start.125
  820.2 4.5 collective-permute-done.123
  840.6 4.5 collective-permute-start.131
  846.5 5.6 collective-permute-done.129
  858.9 4.6 collective-permute-start.133
  866.1 4.5 collective-permute-start.137
  872.1 5.7 collective-permute-done.135
  886.6 9.0 broadcast_in_dim.17
  895.6 10.0 copy.2478
  905.7 4.6 collective-permute-start.139
  911.6 5.6 collective-permute-done.138
  919.7 5.0 collective-permute-start.140
  946.9 4.5 collective-permute-start.146
  974.6 4.5 collective-permute-start.152
  992.5 11.2 %all-reduce.82 = (f32[4]{0:T(128)S(1)}, f32[4]{0:T(128)S(1)}) all-reduce(f32[4]{0:T(128)S(1)} %get-tuple-element.15, f32[4]{0:T(128)S(1)} %get-tuple-element.14), channel_id=1, replica_groups=mesh['gx_0'=4,'gx_1'=2,'gy'=4,'gz'=4] {'gx_0'}, use_global_device_ids=true, to_apply=%region_20.21 | all-reduce | flops 8 | bytes 64 | tf_op jit(solution)/shard_map/psum | solution.py:52
  1006.2 12.6 %all-reduce.80 = (f32[4]{0:T(128)S(1)}, f32[4]{0:T(128)S(1)}) all-reduce(f32[4]{0:T(128)S(1)} %get-tuple-element.30, f32[4]{0:T(128)S(1)} %get-tuple-element.31), channel_id=1, replica_groups=mesh['gx_0'=4,'gx_1'=2,'gy'=4,'gz'=4] {'gy'}, use_global_device_ids=true, to_apply=%region_22.23 | all-reduce | flops 8 | bytes 64 | tf_op jit(solution)/shard_map/psum | solution.py:52
  1018.8 7.7 all-reduce.78
  1028.7 62.0 %psum.135 = f32[4]{0:T(128)S(1)} all-reduce(f32[4]{0:T(128)S(1)} %get-tuple-element.200), channel_id=1, replica_groups=mesh['gx_0'=4,'gx_1'=2,'gy'=4,'gz'=4] {'gx_0','gx_1','gy','gz'}, use_global_device_ids=true, to_apply=%region_30.31 | all-reduce | flops 4 | bytes 32 | tf_op jit(solution)/shard_map/psum | solution.py:202
  (590 shorter events, 462.8 us)
Async XLA Ops:
  30.0 17.3 %collective-permute-start.7 = (f32[4,1,16,128]{3,2,1,0:T(8,128)S(1)}, f32[4,1,16,128]{3,2,1,0:T(8,128)S(1)}, u32[]{:S(2)}, u32[]{:S(2)}) collective-permute-start(f32[4,1,16,128]{3,2,1,0:T(8,128)S(1)} %get-tuple-element.96), channel_id=1, source_target_pairs={{0,16},{16,32},{32,48},{48,64},{64,80},{80,96},{96,112},{1,17},{17... | collective-permute-start | bytes 98312 | tf_op jit(solution)/shard_map/ppermute | solution.py:22
  32.1 15.1 %collective-permute-start.6 = (f32[4,1,16,128]{3,2,1,0:T(8,128)S(1)}, f32[4,1,16,128]{3,2,1,0:T(8,128)S(1)}, u32[]{:S(2)}, u32[]{:S(2)}) collective-permute-start(f32[4,1,16,128]{3,2,1,0:T(8,128)S(1)} %get-tuple-element.97), channel_id=1, source_target_pairs={{16,0},{32,16},{48,32},{64,48},{80,64},{96,80},{112,96},{17,1},{33... | collective-permute-start | bytes 98312 | tf_op jit(solution)/shard_map/ppermute | solution.py:25
  97.4 16.3 %collective-permute-start.13 = (f32[4,1,8,64]{3,2,1,0:T(8,128)S(1)}, f32[4,1,8,64]{3,2,1,0:T(8,128)S(1)}, u32[]{:S(2)}, u32[]{:S(2)}) collective-permute-start(f32[4,1,8,64]{3,2,1,0:T(8,128)S(1)} %get-tuple-element.194), channel_id=1, source_target_pairs={{0,16},{16,32},{32,48},{48,64},{64,80},{80,96},{96,112},{1,17},{17... | collective-permute-start | bytes 24584 | tf_op jit(solution)/shard_map/ppermute | solution.py:38
  114.3 83.5 %collective-permute-start.19 = (f32[4,1,8,64]{3,2,1,0:T(8,128)S(1)}, f32[4,1,8,64]{3,2,1,0:T(8,128)S(1)}, u32[]{:S(2)}, u32[]{:S(2)}) collective-permute-start(f32[4,1,8,64]{3,2,1,0:T(8,128)S(1)} %get-tuple-element.188), channel_id=1, source_target_pairs={{0,16},{16,32},{32,48},{48,64},{64,80},{80,96},{96,112},{1,17},{17... | collective-permute-start | bytes 24584 | tf_op jit(solution)/shard_map/ppermute | solution.py:38
  118.8 78.9 %collective-permute-start.18 = (f32[4,1,8,64]{3,2,1,0:T(8,128)S(1)}, f32[4,1,8,64]{3,2,1,0:T(8,128)S(1)}, u32[]{:S(2)}, u32[]{:S(2)}) collective-permute-start(f32[4,1,8,64]{3,2,1,0:T(8,128)S(1)} %get-tuple-element.189), channel_id=1, source_target_pairs={{16,0},{32,16},{48,32},{64,48},{80,64},{96,80},{112,96},{17,1},{33... | collective-permute-start | bytes 24584 | tf_op jit(solution)/shard_map/ppermute | solution.py:39
  120.1 77.6 %collective-permute-start.22 = (f32[4,8,1,64]{3,2,1,0:T(1,128)S(1)}, f32[4,8,1,64]{3,2,1,0:T(1,128)S(1)}, u32[]{:S(2)}, u32[]{:S(2)}) collective-permute-start(f32[4,8,1,64]{3,2,1,0:T(1,128)S(1)} %get-tuple-element.184), channel_id=1, source_target_pairs={{1,0},{2,1},{3,2},{5,4},{6,5},{7,6},{9,8},{10,9},{11,10},{13,12},{... | collective-permute-start | bytes 24584 | tf_op jit(solution)/shard_map/ppermute | solution.py:39
  121.4 76.3 %collective-permute-start.23 = (f32[4,8,1,64]{3,2,1,0:T(1,128)S(1)}, f32[4,8,1,64]{3,2,1,0:T(1,128)S(1)}, u32[]{:S(2)}, u32[]{:S(2)}) collective-permute-start(f32[4,8,1,64]{3,2,1,0:T(1,128)S(1)} %get-tuple-element.185), channel_id=1, source_target_pairs={{0,1},{1,2},{2,3},{4,5},{5,6},{6,7},{8,9},{9,10},{10,11},{12,13},{... | collective-permute-start | bytes 24584 | tf_op jit(solution)/shard_map/ppermute | solution.py:38
  126.0 66.8 %collective-permute-start.21 = (f32[4,8,8,1]{3,2,1,0:T(8,128)S(1)}, f32[4,8,8,1]{3,2,1,0:T(8,128)S(1)}, u32[]{:S(2)}, u32[]{:S(2)}) collective-permute-start(f32[4,8,8,1]{3,2,1,0:T(8,128)S(1)} %get-tuple-element.186), channel_id=1, source_target_pairs={{4,0},{8,4},{12,8},{5,1},{9,5},{13,9},{6,2},{10,6},{14,10},{7,3},{... | collective-permute-start | bytes 3080 | tf_op jit(solution)/shard_map/ppermute | solution.py:39
  203.3 19.7 %collective-permute-start.25 = (f32[4,1,4,32]{0,3,2,1:T(8,128)S(1)}, f32[4,1,4,32]{0,3,2,1:T(8,128)S(1)}, u32[]{:S(2)}, u32[]{:S(2)}) collective-permute-start(f32[4,1,4,32]{0,3,2,1:T(8,128)S(1)} %get-tuple-element.146), channel_id=1, source_target_pairs={{0,16},{16,32},{32,48},{48,64},{64,80},{80,96},{96,112},{1,17},{17... | collective-permute-start | bytes 6152 | tf_op jit(solution)/shard_map/ppermute | solution.py:38
  204.6 18.4 %collective-permute-start.24 = (f32[4,1,4,32]{0,3,2,1:T(8,128)S(1)}, f32[4,1,4,32]{0,3,2,1:T(8,128)S(1)}, u32[]{:S(2)}, u32[]{:S(2)}) collective-permute-start(f32[4,1,4,32]{0,3,2,1:T(8,128)S(1)} %get-tuple-element.147), channel_id=1, source_target_pairs={{16,0},{32,16},{48,32},{64,48},{80,64},{96,80},{112,96},{17,1},{33... | collective-permute-start | bytes 6152 | tf_op jit(solution)/shard_map/ppermute | solution.py:39
  205.9 17.2 %collective-permute-start.28 = (f32[4,4,1,32]{0,3,2,1:T(8,128)S(1)}, f32[4,4,1,32]{0,3,2,1:T(8,128)S(1)}, u32[]{:S(2)}, u32[]{:S(2)}) collective-permute-start(f32[4,4,1,32]{0,3,2,1:T(8,128)S(1)} %get-tuple-element.142), channel_id=1, source_target_pairs={{1,0},{2,1},{3,2},{5,4},{6,5},{7,6},{9,8},{10,9},{11,10},{13,12},{... | collective-permute-start | bytes 6152 | tf_op jit(solution)/shard_map/ppermute | solution.py:39
  207.2 15.9 %collective-permute-start.29 = (f32[4,4,1,32]{0,3,2,1:T(8,128)S(1)}, f32[4,4,1,32]{0,3,2,1:T(8,128)S(1)}, u32[]{:S(2)}, u32[]{:S(2)}) collective-permute-start(f32[4,4,1,32]{0,3,2,1:T(8,128)S(1)} %get-tuple-element.143), channel_id=1, source_target_pairs={{0,1},{1,2},{2,3},{4,5},{5,6},{6,7},{8,9},{9,10},{10,11},{12,13},{... | collective-permute-start | bytes 6152 | tf_op jit(solution)/shard_map/ppermute | solution.py:38
  223.3 19.6 %collective-permute-start.31 = (f32[4,1,4,32]{0,3,2,1:T(8,128)S(1)}, f32[4,1,4,32]{0,3,2,1:T(8,128)S(1)}, u32[]{:S(2)}, u32[]{:S(2)}) collective-permute-start(f32[4,1,4,32]{0,3,2,1:T(8,128)S(1)} %get-tuple-element.140), channel_id=1, source_target_pairs={{0,16},{16,32},{32,48},{48,64},{64,80},{80,96},{96,112},{1,17},{17... | collective-permute-start | bytes 6152 | tf_op jit(solution)/shard_map/ppermute | solution.py:38
  224.6 18.3 %collective-permute-start.30 = (f32[4,1,4,32]{0,3,2,1:T(8,128)S(1)}, f32[4,1,4,32]{0,3,2,1:T(8,128)S(1)}, u32[]{:S(2)}, u32[]{:S(2)}) collective-permute-start(f32[4,1,4,32]{0,3,2,1:T(8,128)S(1)} %get-tuple-element.141), channel_id=1, source_target_pairs={{16,0},{32,16},{48,32},{64,48},{80,64},{96,80},{112,96},{17,1},{33... | collective-permute-start | bytes 6152 | tf_op jit(solution)/shard_map/ppermute | solution.py:39
  225.9 17.0 %collective-permute-start.34 = (f32[4,4,1,32]{0,3,2,1:T(8,128)S(1)}, f32[4,4,1,32]{0,3,2,1:T(8,128)S(1)}, u32[]{:S(2)}, u32[]{:S(2)}) collective-permute-start(f32[4,4,1,32]{0,3,2,1:T(8,128)S(1)} %get-tuple-element.136), channel_id=1, source_target_pairs={{1,0},{2,1},{3,2},{5,4},{6,5},{7,6},{9,8},{10,9},{11,10},{13,12},{... | collective-permute-start | bytes 6152 | tf_op jit(solution)/shard_map/ppermute | solution.py:39
  227.2 15.7 %collective-permute-start.35 = (f32[4,4,1,32]{0,3,2,1:T(8,128)S(1)}, f32[4,4,1,32]{0,3,2,1:T(8,128)S(1)}, u32[]{:S(2)}, u32[]{:S(2)}) collective-permute-start(f32[4,4,1,32]{0,3,2,1:T(8,128)S(1)} %get-tuple-element.137), channel_id=1, source_target_pairs={{0,1},{1,2},{2,3},{4,5},{5,6},{6,7},{8,9},{9,10},{10,11},{12,13},{... | collective-permute-start | bytes 6152 | tf_op jit(solution)/shard_map/ppermute | solution.py:38
  308.8 18.4 %collective-permute-start.37 = (f32[4,1,4,32]{0,3,2,1:T(8,128)S(1)}, f32[4,1,4,32]{0,3,2,1:T(8,128)S(1)}, u32[]{:S(2)}, u32[]{:S(2)}) collective-permute-start(f32[4,1,4,32]{0,3,2,1:T(8,128)S(1)} %get-tuple-element.134), channel_id=1, source_target_pairs={{0,16},{16,32},{32,48},{48,64},{64,80},{80,96},{96,112},{1,17},{17... | collective-permute-start | bytes 6152 | tf_op jit(solution)/shard_map/ppermute | solution.py:38
  310.2 17.0 %collective-permute-start.36 = (f32[4,1,4,32]{0,3,2,1:T(8,128)S(1)}, f32[4,1,4,32]{0,3,2,1:T(8,128)S(1)}, u32[]{:S(2)}, u32[]{:S(2)}) collective-permute-start(f32[4,1,4,32]{0,3,2,1:T(8,128)S(1)} %get-tuple-element.135), channel_id=1, source_target_pairs={{16,0},{32,16},{48,32},{64,48},{80,64},{96,80},{112,96},{17,1},{33... | collective-permute-start | bytes 6152 | tf_op jit(solution)/shard_map/ppermute | solution.py:39
  311.5 15.7 %collective-permute-start.40 = (f32[4,4,1,32]{0,3,2,1:T(8,128)S(1)}, f32[4,4,1,32]{0,3,2,1:T(8,128)S(1)}, u32[]{:S(2)}, u32[]{:S(2)}) collective-permute-start(f32[4,4,1,32]{0,3,2,1:T(8,128)S(1)} %get-tuple-element.130), channel_id=1, source_target_pairs={{1,0},{2,1},{3,2},{5,4},{6,5},{7,6},{9,8},{10,9},{11,10},{13,12},{... | collective-permute-start | bytes 6152 | tf_op jit(solution)/shard_map/ppermute | solution.py:39
  312.8 14.4 %collective-permute-start.41 = (f32[4,4,1,32]{0,3,2,1:T(8,128)S(1)}, f32[4,4,1,32]{0,3,2,1:T(8,128)S(1)}, u32[]{:S(2)}, u32[]{:S(2)}) collective-permute-start(f32[4,4,1,32]{0,3,2,1:T(8,128)S(1)} %get-tuple-element.131), channel_id=1, source_target_pairs={{0,1},{1,2},{2,3},{4,5},{5,6},{6,7},{8,9},{9,10},{10,11},{12,13},{... | collective-permute-start | bytes 6152 | tf_op jit(solution)/shard_map/ppermute | solution.py:38
  327.6 19.6 %collective-permute-start.43 = (f32[4,1,4,32]{0,3,2,1:T(8,128)S(1)}, f32[4,1,4,32]{0,3,2,1:T(8,128)S(1)}, u32[]{:S(2)}, u32[]{:S(2)}) collective-permute-start(f32[4,1,4,32]{0,3,2,1:T(8,128)S(1)} %get-tuple-element.128), channel_id=1, source_target_pairs={{0,16},{16,32},{32,48},{48,64},{64,80},{80,96},{96,112},{1,17},{17... | collective-permute-start | bytes 6152 | tf_op jit(solution)/shard_map/ppermute | solution.py:38
  328.9 18.3 %collective-permute-start.42 = (f32[4,1,4,32]{0,3,2,1:T(8,128)S(1)}, f32[4,1,4,32]{0,3,2,1:T(8,128)S(1)}, u32[]{:S(2)}, u32[]{:S(2)}) collective-permute-start(f32[4,1,4,32]{0,3,2,1:T(8,128)S(1)} %get-tuple-element.129), channel_id=1, source_target_pairs={{16,0},{32,16},{48,32},{64,48},{80,64},{96,80},{112,96},{17,1},{33... | collective-permute-start | bytes 6152 | tf_op jit(solution)/shard_map/ppermute | solution.py:39
  330.2 17.0 %collective-permute-start.46 = (f32[4,4,1,32]{0,3,2,1:T(8,128)S(1)}, f32[4,4,1,32]{0,3,2,1:T(8,128)S(1)}, u32[]{:S(2)}, u32[]{:S(2)}) collective-permute-start(f32[4,4,1,32]{0,3,2,1:T(8,128)S(1)} %get-tuple-element.124), channel_id=1, source_target_pairs={{1,0},{2,1},{3,2},{5,4},{6,5},{7,6},{9,8},{10,9},{11,10},{13,12},{... | collective-permute-start | bytes 6152 | tf_op jit(solution)/shard_map/ppermute | solution.py:39
  331.5 15.7 %collective-permute-start.47 = (f32[4,4,1,32]{0,3,2,1:T(8,128)S(1)}, f32[4,4,1,32]{0,3,2,1:T(8,128)S(1)}, u32[]{:S(2)}, u32[]{:S(2)}) collective-permute-start(f32[4,4,1,32]{0,3,2,1:T(8,128)S(1)} %get-tuple-element.125), channel_id=1, source_target_pairs={{0,1},{1,2},{2,3},{4,5},{5,6},{6,7},{8,9},{9,10},{10,11},{12,13},{... | collective-permute-start | bytes 6152 | tf_op jit(solution)/shard_map/ppermute | solution.py:38
  352.2 23.7 %collective-permute-start.49 = (f32[4,1,8,64]{3,2,1,0:T(8,128)S(1)}, f32[4,1,8,64]{3,2,1,0:T(8,128)S(1)}, u32[]{:S(2)}, u32[]{:S(2)}) collective-permute-start(f32[4,1,8,64]{3,2,1,0:T(8,128)S(1)} %get-tuple-element.182), channel_id=1, source_target_pairs={{0,16},{16,32},{32,48},{48,64},{64,80},{80,96},{96,112},{1,17},{17... | collective-permute-start | bytes 24584 | tf_op jit(solution)/shard_map/ppermute | solution.py:38
  355.2 20.7 %collective-permute-start.48 = (f32[4,1,8,64]{3,2,1,0:T(8,128)S(1)}, f32[4,1,8,64]{3,2,1,0:T(8,128)S(1)}, u32[]{:S(2)}, u32[]{:S(2)}) collective-permute-start(f32[4,1,8,64]{3,2,1,0:T(8,128)S(1)} %get-tuple-element.183), channel_id=1, source_target_pairs={{16,0},{32,16},{48,32},{64,48},{80,64},{96,80},{112,96},{17,1},{33... | collective-permute-start | bytes 24584 | tf_op jit(solution)/shard_map/ppermute | solution.py:39
  356.5 19.5 %collective-permute-start.52 = (f32[4,8,1,64]{3,2,1,0:T(1,128)S(1)}, f32[4,8,1,64]{3,2,1,0:T(1,128)S(1)}, u32[]{:S(2)}, u32[]{:S(2)}) collective-permute-start(f32[4,8,1,64]{3,2,1,0:T(1,128)S(1)} %get-tuple-element.178), channel_id=1, source_target_pairs={{1,0},{2,1},{3,2},{5,4},{6,5},{7,6},{9,8},{10,9},{11,10},{13,12},{... | collective-permute-start | bytes 24584 | tf_op jit(solution)/shard_map/ppermute | solution.py:39
  358.0 18.0 %collective-permute-start.53 = (f32[4,8,1,64]{3,2,1,0:T(1,128)S(1)}, f32[4,8,1,64]{3,2,1,0:T(1,128)S(1)}, u32[]{:S(2)}, u32[]{:S(2)}) collective-permute-start(f32[4,8,1,64]{3,2,1,0:T(1,128)S(1)} %get-tuple-element.179), channel_id=1, source_target_pairs={{0,1},{1,2},{2,3},{4,5},{5,6},{6,7},{8,9},{9,10},{10,11},{12,13},{... | collective-permute-start | bytes 24584 | tf_op jit(solution)/shard_map/ppermute | solution.py:38
  376.3 25.3 %collective-permute-start.55 = (f32[4,1,8,64]{3,2,1,0:T(8,128)S(1)}, f32[4,1,8,64]{3,2,1,0:T(8,128)S(1)}, u32[]{:S(2)}, u32[]{:S(2)}) collective-permute-start(f32[4,1,8,64]{3,2,1,0:T(8,128)S(1)} %get-tuple-element.176), channel_id=1, source_target_pairs={{0,16},{16,32},{32,48},{48,64},{64,80},{80,96},{96,112},{1,17},{17... | collective-permute-start | bytes 24584 | tf_op jit(solution)/shard_map/ppermute | solution.py:38
  380.9 20.7 %collective-permute-start.54 = (f32[4,1,8,64]{3,2,1,0:T(8,128)S(1)}, f32[4,1,8,64]{3,2,1,0:T(8,128)S(1)}, u32[]{:S(2)}, u32[]{:S(2)}) collective-permute-start(f32[4,1,8,64]{3,2,1,0:T(8,128)S(1)} %get-tuple-element.177), channel_id=1, source_target_pairs={{16,0},{32,16},{48,32},{64,48},{80,64},{96,80},{112,96},{17,1},{33... | collective-permute-start | bytes 24584 | tf_op jit(solution)/shard_map/ppermute | solution.py:39
  382.2 19.4 %collective-permute-start.58 = (f32[4,8,1,64]{3,2,1,0:T(1,128)S(1)}, f32[4,8,1,64]{3,2,1,0:T(1,128)S(1)}, u32[]{:S(2)}, u32[]{:S(2)}) collective-permute-start(f32[4,8,1,64]{3,2,1,0:T(1,128)S(1)} %get-tuple-element.172), channel_id=1, source_target_pairs={{1,0},{2,1},{3,2},{5,4},{6,5},{7,6},{9,8},{10,9},{11,10},{13,12},{... | collective-permute-start | bytes 24584 | tf_op jit(solution)/shard_map/ppermute | solution.py:39
  383.5 18.1 %collective-permute-start.59 = (f32[4,8,1,64]{3,2,1,0:T(1,128)S(1)}, f32[4,8,1,64]{3,2,1,0:T(1,128)S(1)}, u32[]{:S(2)}, u32[]{:S(2)}) collective-permute-start(f32[4,8,1,64]{3,2,1,0:T(1,128)S(1)} %get-tuple-element.173), channel_id=1, source_target_pairs={{0,1},{1,2},{2,3},{4,5},{5,6},{6,7},{8,9},{9,10},{10,11},{12,13},{... | collective-permute-start | bytes 24584 | tf_op jit(solution)/shard_map/ppermute | solution.py:38
  624.3 25.0 %collective-permute-start.91 = (f32[4,1,8,64]{3,2,1,0:T(8,128)S(1)}, f32[4,1,8,64]{3,2,1,0:T(8,128)S(1)}, u32[]{:S(2)}, u32[]{:S(2)}) collective-permute-start(f32[4,1,8,64]{3,2,1,0:T(8,128)S(1)} %get-tuple-element.170), channel_id=1, source_target_pairs={{0,16},{16,32},{32,48},{48,64},{64,80},{80,96},{96,112},{1,17},{17... | collective-permute-start | bytes 24584 | tf_op jit(solution)/shard_map/ppermute | solution.py:38
  626.5 22.7 %collective-permute-start.90 = (f32[4,1,8,64]{3,2,1,0:T(8,128)S(1)}, f32[4,1,8,64]{3,2,1,0:T(8,128)S(1)}, u32[]{:S(2)}, u32[]{:S(2)}) collective-permute-start(f32[4,1,8,64]{3,2,1,0:T(8,128)S(1)} %get-tuple-element.171), channel_id=1, source_target_pairs={{16,0},{32,16},{48,32},{64,48},{80,64},{96,80},{112,96},{17,1},{33... | collective-permute-start | bytes 24584 | tf_op jit(solution)/shard_map/ppermute | solution.py:39
  627.8 21.4 %collective-permute-start.94 = (f32[4,8,1,64]{3,2,1,0:T(1,128)S(1)}, f32[4,8,1,64]{3,2,1,0:T(1,128)S(1)}, u32[]{:S(2)}, u32[]{:S(2)}) collective-permute-start(f32[4,8,1,64]{3,2,1,0:T(1,128)S(1)} %get-tuple-element.166), channel_id=1, source_target_pairs={{1,0},{2,1},{3,2},{5,4},{6,5},{7,6},{9,8},{10,9},{11,10},{13,12},{... | collective-permute-start | bytes 24584 | tf_op jit(solution)/shard_map/ppermute | solution.py:39
  629.1 20.1 %collective-permute-start.95 = (f32[4,8,1,64]{3,2,1,0:T(1,128)S(1)}, f32[4,8,1,64]{3,2,1,0:T(1,128)S(1)}, u32[]{:S(2)}, u32[]{:S(2)}) collective-permute-start(f32[4,8,1,64]{3,2,1,0:T(1,128)S(1)} %get-tuple-element.167), channel_id=1, source_target_pairs={{0,1},{1,2},{2,3},{4,5},{5,6},{6,7},{8,9},{9,10},{10,11},{12,13},{... | collective-permute-start | bytes 24584 | tf_op jit(solution)/shard_map/ppermute | solution.py:38
  649.6 23.6 %collective-permute-start.97 = (f32[4,1,8,64]{3,2,1,0:T(8,128)S(1)}, f32[4,1,8,64]{3,2,1,0:T(8,128)S(1)}, u32[]{:S(2)}, u32[]{:S(2)}) collective-permute-start(f32[4,1,8,64]{3,2,1,0:T(8,128)S(1)} %get-tuple-element.164), channel_id=1, source_target_pairs={{0,16},{16,32},{32,48},{48,64},{64,80},{80,96},{96,112},{1,17},{17... | collective-permute-start | bytes 24584 | tf_op jit(solution)/shard_map/ppermute | solution.py:38
  651.8 21.5 %collective-permute-start.96 = (f32[4,1,8,64]{3,2,1,0:T(8,128)S(1)}, f32[4,1,8,64]{3,2,1,0:T(8,128)S(1)}, u32[]{:S(2)}, u32[]{:S(2)}) collective-permute-start(f32[4,1,8,64]{3,2,1,0:T(8,128)S(1)} %get-tuple-element.165), channel_id=1, source_target_pairs={{16,0},{32,16},{48,32},{64,48},{80,64},{96,80},{112,96},{17,1},{33... | collective-permute-start | bytes 24584 | tf_op jit(solution)/shard_map/ppermute | solution.py:39
  653.1 20.2 %collective-permute-start.100 = (f32[4,8,1,64]{3,2,1,0:T(1,128)S(1)}, f32[4,8,1,64]{3,2,1,0:T(1,128)S(1)}, u32[]{:S(2)}, u32[]{:S(2)}) collective-permute-start(f32[4,8,1,64]{3,2,1,0:T(1,128)S(1)} %get-tuple-element.160), channel_id=1, source_target_pairs={{1,0},{2,1},{3,2},{5,4},{6,5},{7,6},{9,8},{10,9},{11,10},{13,12},{... | collective-permute-start | bytes 24584 | tf_op jit(solution)/shard_map/ppermute | solution.py:39
  654.4 18.9 %collective-permute-start.101 = (f32[4,8,1,64]{3,2,1,0:T(1,128)S(1)}, f32[4,8,1,64]{3,2,1,0:T(1,128)S(1)}, u32[]{:S(2)}, u32[]{:S(2)}) collective-permute-start(f32[4,8,1,64]{3,2,1,0:T(1,128)S(1)} %get-tuple-element.161), channel_id=1, source_target_pairs={{0,1},{1,2},{2,3},{4,5},{5,6},{6,7},{8,9},{9,10},{10,11},{12,13},{... | collective-permute-start | bytes 24584 | tf_op jit(solution)/shard_map/ppermute | solution.py:38
  678.8 21.0 %collective-permute-start.103 = (f32[4,1,4,32]{0,3,2,1:T(8,128)S(1)}, f32[4,1,4,32]{0,3,2,1:T(8,128)S(1)}, u32[]{:S(2)}, u32[]{:S(2)}) collective-permute-start(f32[4,1,4,32]{0,3,2,1:T(8,128)S(1)} %get-tuple-element.122), channel_id=1, source_target_pairs={{0,16},{16,32},{32,48},{48,64},{64,80},{80,96},{96,112},{1,17},{17... | collective-permute-start | bytes 6152 | tf_op jit(solution)/shard_map/ppermute | solution.py:38
  681.6 18.2 %collective-permute-start.102 = (f32[4,1,4,32]{0,3,2,1:T(8,128)S(1)}, f32[4,1,4,32]{0,3,2,1:T(8,128)S(1)}, u32[]{:S(2)}, u32[]{:S(2)}) collective-permute-start(f32[4,1,4,32]{0,3,2,1:T(8,128)S(1)} %get-tuple-element.123), channel_id=1, source_target_pairs={{16,0},{32,16},{48,32},{64,48},{80,64},{96,80},{112,96},{17,1},{33... | collective-permute-start | bytes 6152 | tf_op jit(solution)/shard_map/ppermute | solution.py:39
  682.9 16.9 %collective-permute-start.106 = (f32[4,4,1,32]{0,3,2,1:T(8,128)S(1)}, f32[4,4,1,32]{0,3,2,1:T(8,128)S(1)}, u32[]{:S(2)}, u32[]{:S(2)}) collective-permute-start(f32[4,4,1,32]{0,3,2,1:T(8,128)S(1)} %get-tuple-element.118), channel_id=1, source_target_pairs={{1,0},{2,1},{3,2},{5,4},{6,5},{7,6},{9,8},{10,9},{11,10},{13,12},{... | collective-permute-start | bytes 6152 | tf_op jit(solution)/shard_map/ppermute | solution.py:39
  684.2 15.6 %collective-permute-start.107 = (f32[4,4,1,32]{0,3,2,1:T(8,128)S(1)}, f32[4,4,1,32]{0,3,2,1:T(8,128)S(1)}, u32[]{:S(2)}, u32[]{:S(2)}) collective-permute-start(f32[4,4,1,32]{0,3,2,1:T(8,128)S(1)} %get-tuple-element.119), channel_id=1, source_target_pairs={{0,1},{1,2},{2,3},{4,5},{5,6},{6,7},{8,9},{9,10},{10,11},{12,13},{... | collective-permute-start | bytes 6152 | tf_op jit(solution)/shard_map/ppermute | solution.py:38
  700.1 21.9 %collective-permute-start.109 = (f32[4,1,4,32]{0,3,2,1:T(8,128)S(1)}, f32[4,1,4,32]{0,3,2,1:T(8,128)S(1)}, u32[]{:S(2)}, u32[]{:S(2)}) collective-permute-start(f32[4,1,4,32]{0,3,2,1:T(8,128)S(1)} %get-tuple-element.116), channel_id=1, source_target_pairs={{0,16},{16,32},{32,48},{48,64},{64,80},{80,96},{96,112},{1,17},{17... | collective-permute-start | bytes 6152 | tf_op jit(solution)/shard_map/ppermute | solution.py:38
  704.1 18.0 %collective-permute-start.108 = (f32[4,1,4,32]{0,3,2,1:T(8,128)S(1)}, f32[4,1,4,32]{0,3,2,1:T(8,128)S(1)}, u32[]{:S(2)}, u32[]{:S(2)}) collective-permute-start(f32[4,1,4,32]{0,3,2,1:T(8,128)S(1)} %get-tuple-element.117), channel_id=1, source_target_pairs={{16,0},{32,16},{48,32},{64,48},{80,64},{96,80},{112,96},{17,1},{33... | collective-permute-start | bytes 6152 | tf_op jit(solution)/shard_map/ppermute | solution.py:39
  705.4 16.7 %collective-permute-start.112 = (f32[4,4,1,32]{0,3,2,1:T(8,128)S(1)}, f32[4,4,1,32]{0,3,2,1:T(8,128)S(1)}, u32[]{:S(2)}, u32[]{:S(2)}) collective-permute-start(f32[4,4,1,32]{0,3,2,1:T(8,128)S(1)} %get-tuple-element.112), channel_id=1, source_target_pairs={{1,0},{2,1},{3,2},{5,4},{6,5},{7,6},{9,8},{10,9},{11,10},{13,12},{... | collective-permute-start | bytes 6152 | tf_op jit(solution)/shard_map/ppermute | solution.py:39
  706.7 15.4 %collective-permute-start.113 = (f32[4,4,1,32]{0,3,2,1:T(8,128)S(1)}, f32[4,4,1,32]{0,3,2,1:T(8,128)S(1)}, u32[]{:S(2)}, u32[]{:S(2)}) collective-permute-start(f32[4,4,1,32]{0,3,2,1:T(8,128)S(1)} %get-tuple-element.113), channel_id=1, source_target_pairs={{0,1},{1,2},{2,3},{4,5},{5,6},{6,7},{8,9},{9,10},{10,11},{12,13},{... | collective-permute-start | bytes 6152 | tf_op jit(solution)/shard_map/ppermute | solution.py:38
  791.4 18.7 %collective-permute-start.115 = (f32[4,1,4,32]{0,3,2,1:T(8,128)S(1)}, f32[4,1,4,32]{0,3,2,1:T(8,128)S(1)}, u32[]{:S(2)}, u32[]{:S(2)}) collective-permute-start(f32[4,1,4,32]{0,3,2,1:T(8,128)S(1)} %get-tuple-element.110), channel_id=1, source_target_pairs={{0,16},{16,32},{32,48},{48,64},{64,80},{80,96},{96,112},{1,17},{17... | collective-permute-start | bytes 6152 | tf_op jit(solution)/shard_map/ppermute | solution.py:38
  792.9 17.2 %collective-permute-start.114 = (f32[4,1,4,32]{0,3,2,1:T(8,128)S(1)}, f32[4,1,4,32]{0,3,2,1:T(8,128)S(1)}, u32[]{:S(2)}, u32[]{:S(2)}) collective-permute-start(f32[4,1,4,32]{0,3,2,1:T(8,128)S(1)} %get-tuple-element.111), channel_id=1, source_target_pairs={{16,0},{32,16},{48,32},{64,48},{80,64},{96,80},{112,96},{17,1},{33... | collective-permute-start | bytes 6152 | tf_op jit(solution)/shard_map/ppermute | solution.py:39
  794.2 15.9 %collective-permute-start.118 = (f32[4,4,1,32]{0,3,2,1:T(8,128)S(1)}, f32[4,4,1,32]{0,3,2,1:T(8,128)S(1)}, u32[]{:S(2)}, u32[]{:S(2)}) collective-permute-start(f32[4,4,1,32]{0,3,2,1:T(8,128)S(1)} %get-tuple-element.106), channel_id=1, source_target_pairs={{1,0},{2,1},{3,2},{5,4},{6,5},{7,6},{9,8},{10,9},{11,10},{13,12},{... | collective-permute-start | bytes 6152 | tf_op jit(solution)/shard_map/ppermute | solution.py:39
  795.5 14.7 %collective-permute-start.119 = (f32[4,4,1,32]{0,3,2,1:T(8,128)S(1)}, f32[4,4,1,32]{0,3,2,1:T(8,128)S(1)}, u32[]{:S(2)}, u32[]{:S(2)}) collective-permute-start(f32[4,4,1,32]{0,3,2,1:T(8,128)S(1)} %get-tuple-element.107), channel_id=1, source_target_pairs={{0,1},{1,2},{2,3},{4,5},{5,6},{6,7},{8,9},{9,10},{10,11},{12,13},{... | collective-permute-start | bytes 6152 | tf_op jit(solution)/shard_map/ppermute | solution.py:38
  810.4 19.6 %collective-permute-start.121 = (f32[4,1,4,32]{0,3,2,1:T(8,128)S(1)}, f32[4,1,4,32]{0,3,2,1:T(8,128)S(1)}, u32[]{:S(2)}, u32[]{:S(2)}) collective-permute-start(f32[4,1,4,32]{0,3,2,1:T(8,128)S(1)} %get-tuple-element.104), channel_id=1, source_target_pairs={{0,16},{16,32},{32,48},{48,64},{64,80},{80,96},{96,112},{1,17},{17... | collective-permute-start | bytes 6152 | tf_op jit(solution)/shard_map/ppermute | solution.py:38
  811.7 18.3 %collective-permute-start.120 = (f32[4,1,4,32]{0,3,2,1:T(8,128)S(1)}, f32[4,1,4,32]{0,3,2,1:T(8,128)S(1)}, u32[]{:S(2)}, u32[]{:S(2)}) collective-permute-start(f32[4,1,4,32]{0,3,2,1:T(8,128)S(1)} %get-tuple-element.105), channel_id=1, source_target_pairs={{16,0},{32,16},{48,32},{64,48},{80,64},{96,80},{112,96},{17,1},{33... | collective-permute-start | bytes 6152 | tf_op jit(solution)/shard_map/ppermute | solution.py:39
  813.0 17.0 %collective-permute-start.124 = (f32[4,4,1,32]{0,3,2,1:T(8,128)S(1)}, f32[4,4,1,32]{0,3,2,1:T(8,128)S(1)}, u32[]{:S(2)}, u32[]{:S(2)}) collective-permute-start(f32[4,4,1,32]{0,3,2,1:T(8,128)S(1)} %get-tuple-element.100), channel_id=1, source_target_pairs={{1,0},{2,1},{3,2},{5,4},{6,5},{7,6},{9,8},{10,9},{11,10},{13,12},{... | collective-permute-start | bytes 6152 | tf_op jit(solution)/shard_map/ppermute | solution.py:39
  814.3 15.7 %collective-permute-start.125 = (f32[4,4,1,32]{0,3,2,1:T(8,128)S(1)}, f32[4,4,1,32]{0,3,2,1:T(8,128)S(1)}, u32[]{:S(2)}, u32[]{:S(2)}) collective-permute-start(f32[4,4,1,32]{0,3,2,1:T(8,128)S(1)} %get-tuple-element.101), channel_id=1, source_target_pairs={{0,1},{1,2},{2,3},{4,5},{5,6},{6,7},{8,9},{9,10},{10,11},{12,13},{... | collective-permute-start | bytes 6152 | tf_op jit(solution)/shard_map/ppermute | solution.py:38
  835.0 23.5 %collective-permute-start.127 = (f32[4,1,8,64]{3,2,1,0:T(8,128)S(1)}, f32[4,1,8,64]{3,2,1,0:T(8,128)S(1)}, u32[]{:S(2)}, u32[]{:S(2)}) collective-permute-start(f32[4,1,8,64]{3,2,1,0:T(8,128)S(1)} %get-tuple-element.158), channel_id=1, source_target_pairs={{0,16},{16,32},{32,48},{48,64},{64,80},{80,96},{96,112},{1,17},{17... | collective-permute-start | bytes 24584 | tf_op jit(solution)/shard_map/ppermute | solution.py:38
  838.0 20.5 %collective-permute-start.126 = (f32[4,1,8,64]{3,2,1,0:T(8,128)S(1)}, f32[4,1,8,64]{3,2,1,0:T(8,128)S(1)}, u32[]{:S(2)}, u32[]{:S(2)}) collective-permute-start(f32[4,1,8,64]{3,2,1,0:T(8,128)S(1)} %get-tuple-element.159), channel_id=1, source_target_pairs={{16,0},{32,16},{48,32},{64,48},{80,64},{96,80},{112,96},{17,1},{33... | collective-permute-start | bytes 24584 | tf_op jit(solution)/shard_map/ppermute | solution.py:39
  839.3 19.2 %collective-permute-start.130 = (f32[4,8,1,64]{3,2,1,0:T(1,128)S(1)}, f32[4,8,1,64]{3,2,1,0:T(1,128)S(1)}, u32[]{:S(2)}, u32[]{:S(2)}) collective-permute-start(f32[4,8,1,64]{3,2,1,0:T(1,128)S(1)} %get-tuple-element.154), channel_id=1, source_target_pairs={{1,0},{2,1},{3,2},{5,4},{6,5},{7,6},{9,8},{10,9},{11,10},{13,12},{... | collective-permute-start | bytes 24584 | tf_op jit(solution)/shard_map/ppermute | solution.py:39
  840.6 18.0 %collective-permute-start.131 = (f32[4,8,1,64]{3,2,1,0:T(1,128)S(1)}, f32[4,8,1,64]{3,2,1,0:T(1,128)S(1)}, u32[]{:S(2)}, u32[]{:S(2)}) collective-permute-start(f32[4,8,1,64]{3,2,1,0:T(1,128)S(1)} %get-tuple-element.155), channel_id=1, source_target_pairs={{0,1},{1,2},{2,3},{4,5},{5,6},{6,7},{8,9},{9,10},{10,11},{12,13},{... | collective-permute-start | bytes 24584 | tf_op jit(solution)/shard_map/ppermute | solution.py:38
  858.9 25.3 %collective-permute-start.133 = (f32[4,1,8,64]{3,2,1,0:T(8,128)S(1)}, f32[4,1,8,64]{3,2,1,0:T(8,128)S(1)}, u32[]{:S(2)}, u32[]{:S(2)}) collective-permute-start(f32[4,1,8,64]{3,2,1,0:T(8,128)S(1)} %get-tuple-element.152), channel_id=1, source_target_pairs={{0,16},{16,32},{32,48},{48,64},{64,80},{80,96},{96,112},{1,17},{17... | collective-permute-start | bytes 24584 | tf_op jit(solution)/shard_map/ppermute | solution.py:38
  863.5 20.7 %collective-permute-start.132 = (f32[4,1,8,64]{3,2,1,0:T(8,128)S(1)}, f32[4,1,8,64]{3,2,1,0:T(8,128)S(1)}, u32[]{:S(2)}, u32[]{:S(2)}) collective-permute-start(f32[4,1,8,64]{3,2,1,0:T(8,128)S(1)} %get-tuple-element.153), channel_id=1, source_target_pairs={{16,0},{32,16},{48,32},{64,48},{80,64},{96,80},{112,96},{17,1},{33... | collective-permute-start | bytes 24584 | tf_op jit(solution)/shard_map/ppermute | solution.py:39
  864.8 19.4 %collective-permute-start.136 = (f32[4,8,1,64]{3,2,1,0:T(1,128)S(1)}, f32[4,8,1,64]{3,2,1,0:T(1,128)S(1)}, u32[]{:S(2)}, u32[]{:S(2)}) collective-permute-start(f32[4,8,1,64]{3,2,1,0:T(1,128)S(1)} %get-tuple-element.148), channel_id=1, source_target_pairs={{1,0},{2,1},{3,2},{5,4},{6,5},{7,6},{9,8},{10,9},{11,10},{13,12},{... | collective-permute-start | bytes 24584 | tf_op jit(solution)/shard_map/ppermute | solution.py:39
  866.1 18.1 %collective-permute-start.137 = (f32[4,8,1,64]{3,2,1,0:T(1,128)S(1)}, f32[4,8,1,64]{3,2,1,0:T(1,128)S(1)}, u32[]{:S(2)}, u32[]{:S(2)}) collective-permute-start(f32[4,8,1,64]{3,2,1,0:T(1,128)S(1)} %get-tuple-element.149), channel_id=1, source_target_pairs={{0,1},{1,2},{2,3},{4,5},{5,6},{6,7},{8,9},{9,10},{10,11},{12,13},{... | collective-permute-start | bytes 24584 | tf_op jit(solution)/shard_map/ppermute | solution.py:38
  (102 other events, 798.1 us)
where the time goes:
time: 1110 us; the launch traced here: 1090 us
  starting transfers between devices  375 us (34%)
  blocking collectives  322 us (29%)
  waiting for transfers between devices  201 us (18%)
  local copies, waits for them, and re-layouts  122 us (11%)
  other arithmetic  67.4 us (6%)
    ppermute x48, starting transfers between devices, extended_2(): lax.ppermute(last, axis, up)  174 us
    all_gather x2, blocking collectives, coarsest(): lax.all_gather(rhs_field[None], GX_GY_GZ, axis=0, tiled=True)  126 us
    ppermute x30, starting transfers between devices, extended(): lax.ppermute(lax.slice_in_dim(block, block.shape[dim] - width, None, axis...  99.5 us
    ppermute x30, waiting for transfers between devices, extended(): lax.ppermute(lax.slice_in_dim(block, 0, width, axis=dim), axis, backward)  83.9 us
    ppermute x48, waiting for transfers between devices, extended_2(): lax.ppermute(first, axis, [(b, a) for a, b in up])  69.5 us
    psum x8, blocking collectives, over_axes(): value = lax.psum(value, axis)  68.1 us
    all_gather x1, blocking collectives, per_device(): lax.all_gather(diagonals[LEVELS][None], GX_GY_GZ, axis=0, tiled=True)  65.5 us
    ppermute x48, starting transfers between devices, extended_2(): lax.ppermute(first, axis, [(b, a) for a, b in up])  62.2 us
  transfers between devices with their start and end apart: 156, of which 69 were waited for; matrix products, arithmetic and copies ran while one was open for 2% of the time, Pallas kernels for 0%

commit v1 on v0

v1 whole, which is shorter than its diff:
```python
import functools

import jax
import jax.numpy as jnp
from jax import lax
from jax.experimental import pallas as pl
from jax.experimental.pallas import tpu as pltpu
from jax.sharding import PartitionSpec as P

LEVELS = 3
COARSE_SWEEPS = 8
PROBES = 4
LANES = 128
HALF = 4
MESH = pl.DeviceIdType.MESH
F32 = jnp.float32
HIGHEST = lax.Precision.HIGHEST


def lanes_of(shape):
    return lax.broadcasted_iota(jnp.int32, shape, len(shape) - 1)


def rows_of(shape):
    return lax.broadcasted_iota(jnp.int32, shape, len(shape) - 2)


def turn(value, shift):
    return pltpu.roll(value, shift, len(value.shape) - 1)


def swap_halves(value):
    return pltpu.roll(value, HALF, len(value.shape) - 2)


def kernel_body(
    sizes,
    counts,
    cells,
    kappa_ref,
    bits_ref,
    solution_ref,
    norm_ref,
    *scratch,
):
    names = scratch_names()
    s = dict(zip(names, scratch))
    axes = ("gx", "gz", "gy")
    me = {a: lax.axis_index(a) for a in axes}

    barrier = pltpu.get_barrier_semaphore()
    greeted = 0
    for a in axes:
        for o in range(1, counts[a]):
            pl.semaphore_signal(
                barrier, inc=1, device_id={a: lax.rem(me[a] + o, counts[a])}, device_id_type=MESH
            )
            greeted += 1

    def loop(count, body, init=0, unroll=1):
        return lax.fori_loop(0, count, body, init, unroll=unroll)

    def load_x(x, carry):
        for p in range(PROBES):
            for h in range(2):
                row = h * PROBES + p
                s["flip"][x, pl.ds(row, 8, stride=8), :] = (
                    2.0 * bits_ref[p, x, pl.ds(8 * h, 8), :].astype(F32) - 1.0
                )
        return carry

    loop(16, load_x)

    def take_x(x, carry):
        s["b0"][x] = s["flip"][x].reshape(8, 8, LANES)
        return carry

    loop(16, take_x)

    def kappa_x(x, carry):
        for p in range(PROBES):
            for h in range(2):
                row = h * PROBES + p
                s["flip"][x, pl.ds(row, 8, stride=8), :] = kappa_ref[x, pl.ds(8 * h, 8), :]
        return carry

    loop(16, kappa_x)

    def diag_x(x, carry):
        diag = s["flip"][x].reshape(8, 8, LANES)
        s["d0"][x] = diag + 6.0
        s["w0"][x] = 0.8 / (diag + 6.0)
        return carry

    loop(16, diag_x)

    def coarse_of(field, level):
        xs, zs = field.shape[0] // 2, field.shape[1] // 2
        split = field.reshape(xs, 2, zs, 2, 8, LANES)
        total = (split[:, 0, :, 0] + split[:, 0, :, 1]) + (split[:, 1, :, 0] + split[:, 1, :, 1])
        width = 2**level
        odd = (lanes_of(total.shape) // width) % 2 == 1
        other = jnp.where(odd, turn(total, width), turn(total, LANES - width))
        return 0.125 * (total + other)

    def kappa_coarse(x, carry):
        a = s["flip"][2 * x].reshape(8, 8, LANES)
        b = s["flip"][2 * x + 1].reshape(8, 8, LANES)
        s["e1"][x] = coarse_of(jnp.stack([a, b]), 0)[0]
        return carry

    loop(8, kappa_coarse)
    for level in (1, 2, 3):
        kappa_l = s[f"e{level}"][...]
        s[f"d{level}"][...] = kappa_l + 6.0 * 0.25**level
        s[f"w{level}"][...] = 0.8 / (kappa_l + 6.0 * 0.25**level)
        if level < 3:
            s[f"e{level + 1}"][...] = coarse_of(kappa_l, level)

    for name in names:
        if name[0] in "vr" and name[1] in "0123":
            ref = s[name]
            if name[0] == "v":

                def clear(x, carry, ref=ref):
                    ref[x] = jnp.zeros(ref.shape[1:], F32)
                    return carry

                loop(ref.shape[0], clear)
            else:
                ref[...] = jnp.zeros(ref.shape, F32)
    s["gva"][...] = jnp.zeros(s["gva"].shape, F32)
    s["gvb"][...] = jnp.zeros(s["gvb"].shape, F32)

    pl.semaphore_wait(barrier, greeted)

    def neighbour(a, step):
        return {a: me[a] + step}

    def exchange(level, which):
        xs, zs = sizes[level]
        v = s[f"v{level}{which}"]
        near = s[f"r{level}{which}"]
        pack = s[f"p{level}{which}"]
        yin = s[f"r{level}{which}y"]
        yout = s[f"p{level}{which}y"]
        half = xs // 2
        slot = "abc".index(which)

        first = v[pl.ds(1, xs), 1]
        last = v[pl.ds(1, xs), zs]
        low_rows = rows_of((half, 8, LANES)) < HALF
        pack[0] = jnp.where(low_rows, first[:half], swap_halves(first[half:]))
        pack[1] = jnp.where(low_rows, swap_halves(last[:half]), last[half:])

        def copy(n, src, dst, to):
            return pltpu.make_async_remote_copy(
                src_ref=src,
                dst_ref=dst,
                send_sem=s["send"].at[slot, n],
                recv_sem=s["recv"].at[slot, n],
                device_id=to,
                device_id_type=MESH,
            )

        inner = pl.ds(1, zs)
        plan = []
        for n, (a, step, src, dst) in enumerate(
            (
                ("gz", -1, pack.at[0], near.at[1]),
                ("gz", 1, pack.at[1], near.at[0]),
                ("gx", -1, v.at[1, inner], v.at[xs + 1, inner]),
                ("gx", 1, v.at[xs, inner], v.at[0, inner]),
                ("gy", -1, yout.at[0], yin.at[1]),
                ("gy", 1, yout.at[1], yin.at[0]),
            )
        ):
            there = me[a] > 0 if step < 0 else me[a] < counts[a] - 1
            back = me[a] < counts[a] - 1 if step < 0 else me[a] > 0
            plan.append((there, back, copy(n, src, dst, neighbour(a, step))))
        for there, _, c in plan:
            pl.when(there)(c.start)
        for there, back, c in plan:
            pl.when(back)(c.wait_recv)
        for there, back, c in plan:
            pl.when(there)(c.wait_send)
        low, high = near[0], near[1]
        v[pl.ds(1, half), 0] = jnp.where(low_rows, low, swap_halves(last[:half]))
        v[pl.ds(1 + half, half), 0] = swap_halves(jnp.where(low_rows, last[half:], low))
        v[pl.ds(1, half), zs + 1] = swap_halves(jnp.where(low_rows, high, first[:half]))
        v[pl.ds(1 + half, half), zs + 1] = jnp.where(low_rows, swap_halves(first[half:]), high)

    def y_pack(level, fields, x, carry):
        zs = sizes[level][1]
        width = 2**level
        low, high = carry
        lane = lanes_of((8, LANES))
        for z in range(zs):
            at = (x * zs + z) * width
            moved = turn(fields[z], at)
            low = jnp.where((lane >= at) & (lane < at + width), moved, low)
            before = lax.rem(at + LANES - width, LANES)
            high = jnp.where((lane >= before) & (lane < before + width), moved, high)
        return low, high

    def neighbours(level, which, x):
        xs, zs = sizes[level]
        width = 2**level
        v = s[f"v{level}{which}"]
        yin = s[f"r{level}{which}y"]
        here = v[x + 1, pl.ds(1, zs)]
        total = v[x, pl.ds(1, zs)] + v[x + 2, pl.ds(1, zs)]
        total = total + (v[x + 1, pl.ds(0, zs)] + v[x + 1, pl.ds(2, zs)])
        low, high = yin[0], yin[1]
        lows, highs = [], []
        for z in range(zs):
            at = (x * zs + z) * width
            lows.append(turn(low, lax.rem(2 * LANES + width - at, LANES)))
            highs.append(turn(high, lax.rem(2 * LANES - width - at, LANES)))
        lane = lanes_of((zs, 8, LANES))
        before = jnp.where(lane < width, jnp.stack(lows), turn(here, width))
        after = jnp.where(lane >= LANES - width, jnp.stack(highs), turn(here, LANES - width))
        return here, total + (before + after)

    def unrolled(level):
        return {0: 2, 1: 4, 2: 4}[level]

    def put(level, which, row):
        xs, zs = sizes[level]
        v = s[f"v{level}{which}"]

        def body(x, carry):
            value = row(x)
            v[x + 1, pl.ds(1, zs)] = value
            return y_pack(level, value, x, carry)

        zero = jnp.zeros((8, LANES), F32)
        low, high = loop(xs, body, (zero, zero), unrolled(level))
        s[f"p{level}{which}y"][0] = low
        s[f"p{level}{which}y"][1] = high
        exchange(level, which)

    def swept(level, which):
        coupling = 0.25**level

        def row(x):
            here, around = neighbours(level, which, x)
            b, w = s[f"b{level}"][x], s[f"w{level}"][x]
            return 0.2 * here + w * (b + coupling * around)

        return row

    lane = lanes_of((8, LANES))
    to_lane = lanes_of((LANES, LANES))
    from_lane = rows_of((LANES, LANES))

    def all_along(a, buffer, n, base):
        count = counts[a]
        copies = []
        for o in range(1, count):
            to = lax.rem(me[a] + o, count)
            copies.append(
                pltpu.make_async_remote_copy(
                    src_ref=buffer.at[me[a]],
                    dst_ref=buffer.at[me[a]],
                    send_sem=s["gsend"].at[n, base + o],
                    recv_sem=s["grecv"].at[n, base + o],
                    device_id={a: to},
                    device_id_type=MESH,
                )
            )
        for c in copies:
            c.start()
        for c in copies:
            c.wait_recv()
        for c in copies:
            c.wait_send()

    def gather_coarse(field, n):
        packed = jnp.zeros((8, LANES), F32)
        for x in range(2):
            place = (to_lane == 64 * x + 16 * me["gy"] + from_lane // 8) & (from_lane % 8 == 0)
            packed = packed + jnp.dot(
                field[x, 0], place.astype(F32), precision=HIGHEST, preferred_element_type=F32
            )
        s["g1"][n, me["gy"]] = packed
        all_along("gy", s["g1"].at[n], n, 0)
        parts = s["g1"][n]
        s["g2"][n, me["gz"]] = (parts[0] + parts[1]) + (parts[2] + parts[3])
        all_along("gz", s["g2"].at[n], n, 4)
        s["g3"][n, me["gx"]] = s["g2"][n]
        all_along("gx", s["g3"].at[n], n, 8)

    def coarsest(n):
        coupling = 0.25**LEVELS
        nx, nz = counts["gx"], counts["gz"]
        va, vb = s["gva"], s["gvb"]
        va[pl.ds(1, nx), pl.ds(1, nz)] = s["gw"][...] * s["g3"][n]
        shape = (nz, 8, LANES)
        glane, grow = lanes_of(shape), rows_of(shape)

        def sweep(src, dst):
            def body(x, carry):
                here = src[x + 1, pl.ds(1, nz)]
                along_x = turn(
                    here
                    + jnp.where(glane >= 64, src[x, pl.ds(1, nz)], src[x + 2, pl.ds(1, nz)]),
                    64,
                )
                along_z = swap_halves(
                    here
                    + jnp.where(
                        grow >= HALF, src[x + 1, pl.ds(0, nz)], src[x + 1, pl.ds(2, nz)]
                    )
                )
                before = jnp.where(glane % 64 == 0, 0.0, turn(here, 1))
                after = jnp.where(glane % 64 == 63, 0.0, turn(here, LANES - 1))
                around = (along_x + along_z) + (before + after)
                dst[x + 1, pl.ds(1, nz)] = 0.2 * here + s["gw"][x] * (
                    s["g3"][n, x] + coupling * around
                )
                return carry

            loop(nx, body, 0, 4)

        for i in range(COARSE_SWEEPS - 1):
            sweep(*((va, vb) if i % 2 == 0 else (vb, va)))
        done = vb if (COARSE_SWEEPS - 1) % 2 else va
        mine = done[1 + me["gx"], 1 + me["gz"]]
        for x in range(2):
            place = from_lane == 64 * x + 16 * me["gy"] + to_lane // 8
            s["e3"][x, 0] = jnp.dot(
                mine, place.astype(F32), precision=HIGHEST, preferred_element_type=F32
            )

    def down(level):
        xs, zs = sizes[level]
        coupling = 0.25**level
        put(level, "a", lambda x: s[f"w{level}"][x] * s[f"b{level}"][x])
        put(level, "b", swept(level, "a"))

        def remainder(x):
            here, around = neighbours(level, "b", x)
            return s[f"b{level}"][x] - (s[f"d{level}"][x] * here - coupling * around)

        def body(x, carry):
            fine = jnp.stack([remainder(2 * x), remainder(2 * x + 1)])
            s[f"b{level + 1}"][x] = coarse_of(fine, level)[0]
            return carry

        loop(xs // 2, body)

    def up(level):
        xs, zs = sizes[level]
        v = s[f"v{level}b"]

        def corrected(x):
            e = s[f"e{level + 1}"][x // 2]
            e = jnp.stack([e, e], axis=1).reshape(zs, 8, LANES)
            return v[x + 1, pl.ds(1, zs)] + e

        put(level, "a", corrected)
        put(level, "b", swept(level, "a"))

    def cycle(n):
        for level in range(LEVELS):
            down(level)
        gather_coarse(s["b3"][...], n + 1)
        coarsest(n + 1)
        for level in (2, 1):
            up(level)
            row = swept(level, "b")

            def body(x, carry, level=level, row=row):
                s[f"e{level}"][x] = row(x)
                return carry

            loop(sizes[level][0], body, 0, unrolled(level))
        up(0)
        put(0, "c", swept(0, "b"))

    gather_coarse(s["d3"][...], 0)
    gdiag = s["g3"][0]
    s["gw"][...] = 0.8 / gdiag

    def iterate(n, carry):
        cycle(n)

        def apply(x, c):
            here, around = neighbours(0, "c", x)
            q = s["d0"][x] * here - around
            s["z"][n, x] = here
            s["q"][n, x] = q

            @pl.when(n == 0)
            def _():
                s["flip"][x] = s["b0"][x].reshape(64, LANES)

            s["b0"][x] = q
            return c

        loop(16, apply)
        return carry

    loop(2, iterate)

    def reduce_all(dots, n):
        packed = jnp.zeros((8, LANES), F32)
        for j, d in enumerate(dots):
            total = jnp.sum(d, axis=-1, keepdims=True)
            packed = jnp.where(lane == j, total, packed)
        packed = packed + swap_halves(packed)
        s["a1"][n, me["gy"]] = packed
        all_along("gy", s["a1"].at[n], n, 16)
        parts = s["a1"][n]
        s["a2"][n, me["gz"]] = (parts[0] + parts[1]) + (parts[2] + parts[3])
        all_along("gz", s["a2"].at[n], n, 20)
        parts = s["a2"][n]
        s["a3"][n, me["gx"]] = (parts[0] + parts[1]) + (parts[2] + parts[3])
        all_along("gx", s["a3"].at[n], n, 24)
        parts = s["a3"][n]
        parts = (parts[:4] + parts[4:])
        total = (parts[0] + parts[1]) + (parts[2] + parts[3])
        return [total[:, j : j + 1] for j in range(len(dots))]

    zero = jnp.zeros((8, LANES), F32)

    def folded(value):
        while value.shape[0] > 1:
            value = value[: value.shape[0] // 2] + value[value.shape[0] // 2 :]
        return value[0]

    def dots_first(x, c):
        b = s["flip"][x].reshape(8, 8, LANES)
        z = s["z"][0, x]
        return c[0] + folded(b * z), c[1] + folded(z * s["q"][0, x])

    rz, zq = reduce_all(loop(16, dots_first, (zero, zero)), 0)
    step = jnp.broadcast_to(rz / zq, (8, LANES))

    def dots_second(x, c):
        q0 = s["q"][0, x]
        z0 = s["z"][0, x]
        r1 = s["flip"][x].reshape(8, 8, LANES) - step * q0
        z1 = z0 - step * s["z"][1, x]
        q1 = q0 - step * s["q"][1, x]
        s["z"][1, x] = z1
        pairs = ((r1, z1), (z1, q1), (z1, q0), (z0, q1), (r1, r1), (r1, q1), (r1, q0), (q1, q1), (q1, q0), (q0, q0))
        return tuple(t + folded(u * v) for t, (u, v) in zip(c, pairs))

    r1z1, z1q1, z1q0, z0q1, r1r1, r1q1, r1q0, q1q1, q1q0, q0q0 = reduce_all(
        loop(16, dots_second, (zero,) * 10), 1
    )
    ratio = r1z1 / rz
    step2 = r1z1 / (z1q1 + ratio * (z1q0 + z0q1) + ratio * ratio * zq)
    squares = (
        r1r1
        - 2.0 * step2 * (r1q1 + ratio * r1q0)
        + step2 * step2 * (q1q1 + 2.0 * ratio * q1q0 + ratio * ratio * q0q0)
    )
    norm = jnp.sqrt(jnp.maximum(squares, 0.0) * (1.0 / cells))
    norm_ref[...] = jnp.broadcast_to(norm, (8, LANES))
    along_z0 = jnp.broadcast_to(step + step2 * ratio, (8, LANES))
    along_z1 = jnp.broadcast_to(step2, (8, LANES))

    def finish(x, c):
        value = along_z0 * s["z"][0, x] + along_z1 * s["z"][1, x]
        s["flip"][x] = value.reshape(64, LANES)
        return c

    loop(16, finish)

    def write(x, c):
        for p in range(PROBES):
            for h in range(2):
                row = h * PROBES + p
                solution_ref[p, x, pl.ds(8 * h, 8), :] = s["flip"][x, pl.ds(row, 8, stride=8), :]
        return c

    loop(16, write)


SIZES = ((16, 8), (8, 4), (4, 2), (2, 1))


def scratch_list():
    out = {"flip": pltpu.VMEM((16, 64, LANES), F32)}
    for level, (xs, zs) in enumerate(SIZES):
        for name in "bdwe":
            out[f"{name}{level}"] = pltpu.VMEM((xs, zs, 8, LANES), F32)
        if level == LEVELS:
            continue
        for which in "abc" if level == 0 else "ab":
            out[f"v{level}{which}"] = pltpu.VMEM((xs + 2, zs + 2, 8, LANES), F32)
            out[f"r{level}{which}"] = pltpu.VMEM((2, xs // 2, 8, LANES), F32)
            out[f"p{level}{which}"] = pltpu.VMEM((2, xs // 2, 8, LANES), F32)
            out[f"r{level}{which}y"] = pltpu.VMEM((2, 8, LANES), F32)
            out[f"p{level}{which}y"] = pltpu.VMEM((2, 8, LANES), F32)
    out["z"] = pltpu.VMEM((2, 16, 8, 8, LANES), F32)
    out["q"] = pltpu.VMEM((2, 16, 8, 8, LANES), F32)
    out["g1"] = pltpu.VMEM((3, 4, 8, LANES), F32)
    out["g2"] = pltpu.VMEM((3, 4, 8, LANES), F32)
    out["g3"] = pltpu.VMEM((3, 8, 4, 8, LANES), F32)
    out["a1"] = pltpu.VMEM((2, 4, 8, LANES), F32)
    out["a2"] = pltpu.VMEM((2, 4, 8, LANES), F32)
    out["a3"] = pltpu.VMEM((2, 8, 8, LANES), F32)
    out["gw"] = pltpu.VMEM((8, 4, 8, LANES), F32)
    out["gva"] = pltpu.VMEM((10, 6, 8, LANES), F32)
    out["gvb"] = pltpu.VMEM((10, 6, 8, LANES), F32)
    out["send"] = pltpu.SemaphoreType.DMA((3, 6))
    out["recv"] = pltpu.SemaphoreType.DMA((3, 6))
    out["gsend"] = pltpu.SemaphoreType.DMA((3, 32))
    out["grecv"] = pltpu.SemaphoreType.DMA((3, 32))
    return out


def scratch_names():
    return list(scratch_list())


def solution(mesh):
    counts = {a: mesh.shape[a] for a in ("gx", "gy", "gz")}

    def step(kappa_sq, probe_bits):
        cells = probe_bits[0].size * counts["gx"] * counts["gy"] * counts["gz"]
        whole, norms = pl.pallas_call(
            functools.partial(kernel_body, SIZES, counts, cells),
            out_shape=(
                jax.ShapeDtypeStruct(probe_bits.shape, F32),
                jax.ShapeDtypeStruct((8, LANES), F32),
            ),
            in_specs=[pl.BlockSpec(memory_space=pltpu.VMEM)] * 2,
            out_specs=(pl.BlockSpec(memory_space=pltpu.VMEM),) * 2,
            scratch_shapes=list(scratch_list().values()),
            compiler_params=pltpu.CompilerParams(
                collective_id=0, has_side_effects=True, vmem_limit_bytes=40 * 2**20
            ),
            name="solve",
        )(kappa_sq, probe_bits)
        return whole, norms[:PROBES, 0]

    return jax.shard_map(
        step,
        mesh=mesh,
        in_specs=(P("gx", "gz", "gy"), P(None, "gx", "gz", "gy")),
        out_specs=(P(None, "gx", "gz", "gy"), P()),
        check_vma=False,
    )
```

time: 1110 us -> 175 us (0.16); the launches traced: 1090 us -> 174 us
  starting transfers between devices: 375 us -> 0 us
  blocking collectives: 322 us -> 0 us
  waiting for transfers between devices: 201 us -> 0 us
  Pallas kernels: 0 us -> 170 us
  local copies, waits for them, and re-layouts: 122 us -> 3.36 us
  other arithmetic: 67.4 us -> 0 us
    ppermute x156 -> x0, starting transfers between devices: 375 us -> none  [the longest x48 174 us: extended_2(): lax.ppermute(last, axis, up)]
    ppermute x156 -> x0, waiting for transfers between devices: 201 us -> none  [the longest x30 83.9 us: extended(): lax.ppermute(lax.slice_in_dim(block, 0, width, axis=dim), axis, backward)]
    all_gather x3 -> x0, blocking collectives: 192 us -> none  [the longest x2 126 us: coarsest(): lax.all_gather(rhs_field[None], GX_GY_GZ, axis=0, tiled=True)]
    pallas_call x0 -> x1, Pallas kernels: none -> 170 us  [step(): pl.pallas_call(functools.partial(kernel_body, SIZES, counts, cells), out_...]
    psum x9 -> x0, blocking collectives: 130 us -> none  [the longest x8 68.1 us: over_axes(): value = lax.psum(value, axis)]
    reduce_sum x12 -> x0, other arithmetic: 41.5 us -> none  [the longest x9 36.7 us: coarsen(): return jnp.mean(grouped, axis=(-5, -3, -1))]
    reshape x7 -> x0, local copies, waits for them, and re-layouts: 36.4 us -> none  [the longest x4 24.6 us: refine(): spread.reshape(leading + (cells_first * 2, cells_second * 2, cells_third...]
    broadcast_in_dim x6 -> x0, local copies, waits for them, and re-layouts: 23 us -> none  [refine(): jnp.broadcast_to(spread, leading + (cells_first, 2, cells_second, 2, cell...]
  transfers between devices with their start and end apart: 156 -> 0, of which waited for: 69 -> 0; matrix products, arithmetic and copies ran while one was open for 2% -> 0% of each run, Pallas kernels for 0% -> 0%
where the time goes in v1:
time: 175 us; the launch traced here: 174 us
  Pallas kernels  170 us (97%)
  local copies, waits for them, and re-layouts  3.36 us (2%)
    pallas_call x1, Pallas kernels, step(): pl.pallas_call(functools.partial(kernel_body, SIZES, counts, cells), out_...  170 us

profile of v1, /device:TPU:0, one launch (start us, length us, event | category | flops | bytes accessed | tf_op | source)
XLA Modules:
  0.0 173.9 jit_solution(148140393131487554)
XLA Ops:
  0.6 0.0 copy-start
  0.6 1.0 copy-done
  1.7 0.0 copy-start.1
  1.7 0.9 copy-done.1
  2.6 169.9 %solve.1 = (f32[4,16,16,128]{3,2,1,0:T(8,128)S(1)}, f32[8,128]{1,0:T(8,128)S(1)}) custom-call(f32[16,16,128]{2,1,0:T(8,128)S(1)} %copy-done.1, s32[4,16,16,128]{3,2,1,0:T(8,128)S(1)} %copy-done), custom_call_target="tpu_custom_call" | custom-call | tf_op jit(solution)/shard_map/solve/pallas_call | solution.py:526
  172.5 0.6 slice_reduce_fusion
  173.1 0.8 copy.5
Async XLA Ops:
  0.6 1.0 copy-start
  1.7 0.9 copy-start.1

commit v2 on v1

v2 whole, which is shorter than its diff:
```python
import functools

import jax
import jax.numpy as jnp
from jax import lax
from jax.experimental import pallas as pl
from jax.experimental.pallas import tpu as pltpu
from jax.sharding import PartitionSpec as P

LEVELS = 3
COARSE_SWEEPS = 8
PROBES = 4
LANES = 128
HALF = 4
MESH = pl.DeviceIdType.MESH
F32 = jnp.float32
HIGHEST = lax.Precision.HIGHEST

OWN = {1: 32, 2: 48, 3: 24}
REACH = {1: 3, 2: 4}


def lanes_of(shape):
    return lax.broadcasted_iota(jnp.int32, shape, len(shape) - 1)


def rows_of(shape):
    return lax.broadcasted_iota(jnp.int32, shape, len(shape) - 2)


def turn(value, shift):
    return pltpu.roll(value, shift, len(value.shape) - 1)


def swap_halves(value):
    return pltpu.roll(value, HALF, len(value.shape) - 2)


def kernel_body(counts, cells, kappa_ref, bits_ref, solution_ref, norm_ref, *scratch):
    s = dict(zip(scratch_list(), scratch))
    axes = ("gx", "gz", "gy")
    me = {a: lax.axis_index(a) for a in axes}
    nx, nz = counts["gx"], counts["gz"]
    lane = lanes_of((8, LANES))

    def loop(count, body, init=0, unroll=1):
        return lax.fori_loop(0, count, body, init, unroll=unroll)

    def exists(steps):
        ok = None
        for a, d in zip(axes, steps):
            if d:
                one = me[a] > 0 if d < 0 else me[a] < counts[a] - 1
                ok = one if ok is None else ok & one
        return ok

    def device(steps):
        return {a: me[a] + d for a, d in zip(axes, steps)}

    around_me = [
        (i, j, k) for i in (-1, 0, 1) for j in (-1, 0, 1) for k in (-1, 0, 1) if (i, j, k) != (0, 0, 0)
    ]

    for which in "abc":
        ref = s[f"v0{which}"]
        for x in (0, 17):
            ref[x] = jnp.zeros(ref.shape[1:], F32)
        for name in (f"r0{which}", f"r0{which}y"):
            s[name][...] = jnp.zeros(s[name].shape, F32)
    for name in ("m1", "y1", "m2"):
        ref = s[name]

        def clear(i, carry, ref=ref):
            for j in range(3):
                ref[i // 3, lax.rem(i, 3), j] = jnp.zeros(ref.shape[3:], F32)
            return carry

        loop(9, clear)
    for name in ("gva", "gvb"):
        s[name][...] = jnp.zeros(s[name].shape, F32)

    barrier = pltpu.get_barrier_semaphore()

    def greet(to):
        pl.semaphore_signal(barrier, inc=1, device_id=to, device_id_type=MESH)

    def plane_peer(o):
        i, j = o // nz, lax.rem(o, nz)
        return {"gx": lax.rem(me["gx"] + i, nx), "gz": lax.rem(me["gz"] + j, nz)}

    def greet_plane(o, carry):
        greet(plane_peer(o + 1))
        return carry

    loop(nx * nz - 1, greet_plane)
    for o in range(1, counts["gy"]):
        greet({"gy": lax.rem(me["gy"] + o, counts["gy"])})
    for steps in around_me:
        if steps[2] and steps[:2] != (0, 0):
            pl.when(exists(steps))(functools.partial(greet, device(steps)))
    near = {
        a: (me[a] > 0).astype(jnp.int32) + (me[a] < counts[a] - 1).astype(jnp.int32) for a in axes
    }
    greeted = (
        nx * nz - 1 + counts["gy"] - 1 + ((near["gx"] + 1) * (near["gz"] + 1) - 1) * near["gy"]
    )

    row_at = rows_of((LANES, LANES))
    col_at = lanes_of((LANES, LANES))

    def halved(value):
        return (value + 256) // 2 - 128

    def keep(name, where, weight):
        s["lanes"][MATRICES.index(name)] = jnp.where(where, weight, 0.0)

    keep("c01", col_at == 32 + row_at // 2, 0.125)
    keep("c12", (col_at == 48 + halved(row_at - 32)) & (row_at >= 32) & (row_at < 96), 0.125)
    inside = (row_at >= 18) & (row_at < 110)
    keep("p10", row_at == 32 + col_at // 2, 1.0)
    keep("p21", row_at == 48 + halved(col_at - 32), 1.0)
    for i in range(2):
        keep(f"c23{i}", (col_at == 64 * i + 24 + halved(row_at - 48)) & inside, 0.125)
        keep(f"p32{i}", row_at == 64 * i + 24 + halved(col_at - 48), 1.0)

    def moved(value, name):
        shape = value.shape
        flat = jnp.dot(
            value.reshape(-1, LANES),
            s["lanes"][MATRICES.index(name)],
            precision=HIGHEST,
            preferred_element_type=F32,
        )
        return flat.reshape(shape)

    def load_x(x, carry):
        for p in range(PROBES):
            for h in range(2):
                row = h * PROBES + p
                s["flip"][x, pl.ds(row, 8, stride=8), :] = (
                    2.0 * bits_ref[p, x, pl.ds(8 * h, 8), :].astype(F32) - 1.0
                )
        return carry

    def take_x(x, carry):
        s["b0"][x] = s["flip"][x].reshape(8, 8, LANES)
        return carry

    def kappa_x(x, carry):
        for p in range(PROBES):
            for h in range(2):
                row = h * PROBES + p
                s["flip"][x, pl.ds(row, 8, stride=8), :] = kappa_ref[x, pl.ds(8 * h, 8), :]
        return carry

    def pair_sum(field):
        xs, zs = field.shape[0] // 2, field.shape[1] // 2
        split = field.reshape(xs, 2, zs, 2, 8, LANES)
        return (split[:, 0, :, 0] + split[:, 0, :, 1]) + (split[:, 1, :, 0] + split[:, 1, :, 1])

    def diag_x(x, carry):
        kappas = [s["flip"][2 * x + i].reshape(8, 8, LANES) for i in range(2)]
        for i in range(2):
            s["d0"][2 * x + i] = kappas[i] + 6.0
            s["w0"][2 * x + i] = 0.8 / (kappas[i] + 6.0)
        s["t1"][x] = pair_sum(jnp.stack(kappas))[0]
        return carry

    loop(16, load_x)
    loop(16, take_x)
    loop(16, kappa_x)
    loop(8, diag_x)

    def exchange(which):
        v = s[f"v0{which}"]
        got = s[f"r0{which}"]
        pack = s[f"p0{which}"]
        yin = s[f"r0{which}y"]
        yout = s[f"p0{which}y"]
        slot = "abc".index(which)
        first = v[pl.ds(1, 16), 1]
        last = v[pl.ds(1, 16), 8]
        low_rows = rows_of((8, 8, LANES)) < HALF
        pack[0] = jnp.where(low_rows, first[:8], swap_halves(first[8:]))
        pack[1] = jnp.where(low_rows, swap_halves(last[:8]), last[8:])
        inner = pl.ds(1, 8)
        plan = []
        for n, (steps, src, dst) in enumerate(
            (
                ((0, -1, 0), pack.at[0], got.at[1]),
                ((0, 1, 0), pack.at[1], got.at[0]),
                ((-1, 0, 0), v.at[1, inner], v.at[17, inner]),
                ((1, 0, 0), v.at[16, inner], v.at[0, inner]),
                ((0, 0, -1), yout.at[0], yin.at[1]),
                ((0, 0, 1), yout.at[1], yin.at[0]),
            )
        ):
            c = pltpu.make_async_remote_copy(
                src_ref=src,
                dst_ref=dst,
                send_sem=s["send"].at[slot, n],
                recv_sem=s["recv"].at[slot, n],
                device_id=device(steps),
                device_id_type=MESH,
            )
            plan.append((exists(steps), exists(tuple(-d for d in steps)), c))
        for there, _, c in plan:
            pl.when(there)(c.start)
        for _, back, c in plan:
            pl.when(back)(c.wait_recv)
        for there, _, c in plan:
            pl.when(there)(c.wait_send)
        low, high = got[0], got[1]
        v[pl.ds(1, 8), 0] = jnp.where(low_rows, low, swap_halves(last[:8]))
        v[pl.ds(9, 8), 0] = swap_halves(jnp.where(low_rows, last[8:], low))
        v[pl.ds(1, 8), 9] = swap_halves(jnp.where(low_rows, high, first[:8]))
        v[pl.ds(9, 8), 9] = jnp.where(low_rows, swap_halves(first[8:]), high)

    def y_pack(fields, x, carry):
        low, high = carry
        for z in range(8):
            at = x * 8 + z
            turned = turn(fields[z], at)
            low = jnp.where(lane == at, turned, low)
            high = jnp.where(lane == lax.rem(at + LANES - 1, LANES), turned, high)
        return low, high

    def neighbours(which, x):
        v = s[f"v0{which}"]
        yin = s[f"r0{which}y"]
        here = v[x + 1, pl.ds(1, 8)]
        total = v[x, pl.ds(1, 8)] + v[x + 2, pl.ds(1, 8)]
        total = total + (v[x + 1, pl.ds(0, 8)] + v[x + 1, pl.ds(2, 8)])
        low, high = yin[0], yin[1]
        lows, highs = [], []
        for z in range(8):
            at = x * 8 + z
            lows.append(turn(low, lax.rem(2 * LANES + 1 - at, LANES)))
            highs.append(turn(high, lax.rem(2 * LANES - 1 - at, LANES)))
        at_lane = lanes_of((8, 8, LANES))
        before = jnp.where(at_lane < 1, jnp.stack(lows), turn(here, 1))
        after = jnp.where(at_lane >= LANES - 1, jnp.stack(highs), turn(here, LANES - 1))
        return here, total + (before + after)

    def put(which, row):
        v = s[f"v0{which}"]

        def body(x, carry):
            value = row(x)
            v[x + 1, pl.ds(1, 8)] = value
            return y_pack(value, x, carry)

        zero = jnp.zeros((8, LANES), F32)
        low, high = loop(16, body, (zero, zero), 2)
        s[f"p0{which}y"][0] = low
        s[f"p0{which}y"][1] = high
        exchange(which)

    def swept(which):
        def row(x):
            here, around = neighbours(which, x)
            return 0.2 * here + s["w0"][x] * (s["b0"][x] + around)

        return row

    def start_exchange(level, n, field):
        if level == 1:
            pack = s["m1"].at[n, 1, 1]
            pairs = field.reshape(4, 2, 4, 8, LANES)
            pack[...] = turn(pairs[:, 0], LANES - 32) + turn(pairs[:, 1], 32)
            low = high = jnp.zeros((8, LANES), F32)
            for x in range(8):
                for z in range(4):
                    at = 4 * (4 * x + z)
                    slot = (lane >= at) & (lane < at + 4)
                    low = jnp.where(slot, turn(field[x, z], (at + 2 * LANES - 32) % LANES), low)
                    high = jnp.where(slot, turn(field[x, z], (at + 2 * LANES - 92) % LANES), high)
            s["y1out"][n, 0] = high
            s["y1out"][n, 1] = low
        else:
            pack = s["m2"].at[n, 1, 1, 1]
            total = turn(field[0], LANES - 48)
            for x in range(1, 4):
                total = total + turn(field[x], (32 * x + LANES - 48) % LANES)
            pack[...] = total
        plan = exchange_plan(level, n)
        for there, _, c in plan:
            pl.when(there)(c.start)
        return plan

    def exchange_plan(level, n):
        plan = []
        for steps in around_me:
            i, j, k = steps
            if level == 2:
                src = s["m2"].at[n, 1, 1, 1]
                dst = s["m2"].at[n, 1 - i, 1 - j, 1 - k]
            elif k:
                side = 0 if k > 0 else 1
                src = s["y1out"].at[n, side]
                dst = s["y1"].at[n, 1 - i, 1 - j, side]
            else:
                if j == 0:
                    part = (pl.ds(0 if i < 0 else 2, 2),)
                elif i == 0:
                    part = (slice(None), pl.ds(0 if j < 0 else 1, 3))
                else:
                    part = (pl.ds(0 if i < 0 else 3, 1), pl.ds(0 if j < 0 else 2, 2))
                src = s["m1"].at[(n, 1, 1, *part)]
                dst = s["m1"].at[(n, 1 - i, 1 - j, *part)]
            at = 9 * (i + 1) + 3 * (j + 1) + (k + 1)
            c = pltpu.make_async_remote_copy(
                src_ref=src,
                dst_ref=dst,
                send_sem=s["xsend"].at[level - 1, n, at],
                recv_sem=s["xrecv"].at[level - 1, n, at],
                device_id=device(steps),
                device_id_type=MESH,
            )
            plan.append((exists(steps), exists(tuple(-d for d in steps)), c))
        return plan

    def finish_exchange(level, n, plan, out):
        for _, back, c in plan:
            pl.when(back)(c.wait_recv)
        for there, _, c in plan:
            pl.when(there)(c.wait_send)
        low_rows = rows_of((8, LANES)) < HALF
        reach = REACH[level]
        xs, zs = (8, 4) if level == 1 else (4, 2)

        def body(x, carry):
            far = (x + xs - reach) // xs
            at_x = lax.rem(x + xs - reach, xs)

            def source(j, z):
                if level == 1:
                    mid = turn(
                        s["m1"][n, far, j, at_x // 2, z], 32 + 64 * lax.rem(at_x, 2)
                    )
                    at = 4 * (4 * at_x + z)
                    left = turn(s["y1"][n, far, j, 0], lax.rem(28 - at + 2 * LANES, LANES))
                    right = turn(s["y1"][n, far, j, 1], lax.rem(96 - at + 2 * LANES, LANES))
                    value = jnp.where((lane >= 28) & (lane < 32), left, 0.0)
                    value = jnp.where((lane >= 96) & (lane < 100), right, value)
                    return jnp.where((lane >= 32) & (lane < 96), mid, value)
                value = jnp.zeros((8, LANES), F32)
                for k in range(3):
                    start = 16 + 32 * k
                    part = turn(
                        s["m2"][n, far, j, k, z], lax.rem(start + 2 * LANES - 32 * at_x, LANES)
                    )
                    value = jnp.where((lane >= start) & (lane < start + 32), part, value)
                return value

            mine = [source(1, z) for z in range(zs)]
            if level == 1:
                down = [None] + [source(0, z) for z in (1, 2, 3)]
                over = [source(2, z) for z in (0, 1, 2)]
                below = [(down[z], mine[z]) for z in (1, 2, 3)]
                above = [(over[z], mine[z]) for z in (0, 1, 2)]
                outer_low, outer_high = [], []
            else:
                outer_low = [source(0, z) for z in range(2)]
                outer_high = [source(2, z) for z in range(2)]
                below = list(zip(outer_low, mine))
                above = list(zip(outer_high, mine))
            values = list(outer_low)
            values += [swap_halves(jnp.where(low_rows, own, other)) for other, own in below]
            values += mine
            values += [swap_halves(jnp.where(low_rows, other, own)) for other, own in above]
            values += outer_high
            out[x] = jnp.stack(values)
            return carry

        loop(xs + 2 * reach, body)

    def held_row(src, x, z0, z1):
        inner = pl.ds(z0, z1 - z0)
        here = src[x, inner]
        total = (src[x - 1, inner] + src[x + 1, inner]) + (
            src[x, pl.ds(z0 - 1, z1 - z0)] + src[x, pl.ds(z0 + 1, z1 - z0)]
        )
        return here, total + (turn(here, 1) + turn(here, LANES - 1))

    def held_sweep(level, src, dst, margin, into=0):
        xs, zs = s[f"b{level}"].shape[:2]
        coupling = 0.25**level
        z0, z1 = margin, zs - margin

        def body(i, carry):
            x = i + margin
            here, around = held_row(src, x, z0, z1)
            inner = pl.ds(z0, z1 - z0)
            value = 0.2 * here + s[f"w{level}"][x, inner] * (
                s[f"b{level}"][x, inner] + coupling * around
            )
            if into:
                dst[i] = value
            else:
                dst[x, inner] = value
            return carry

        loop(xs - 2 * margin, body, 0, 2)

    def held_down(level):
        xs, zs = s[f"b{level}"].shape[:2]
        reach = REACH[level]
        coupling = 0.25**level

        def begin(x, carry):
            s[f"v{level}a"][x] = s[f"w{level}"][x] * s[f"b{level}"][x]
            return carry

        loop(xs, begin)
        held_sweep(level, s[f"v{level}a"], s[f"v{level}b"], 1)
        z0, z1 = reach, zs - reach
        own = []
        for x in range(reach, xs - reach):
            here, around = held_row(s[f"v{level}b"], x, z0, z1)
            inner = pl.ds(z0, z1 - z0)
            own.append(
                s[f"b{level}"][x, inner] - (s[f"d{level}"][x - reach] * here - coupling * around)
            )
        return jnp.stack(own)

    def held_up(level, coarse, spread, out, last_margin):
        xs, zs = s[f"b{level}"].shape[:2]

        def add(i, carry):
            x = i + 1
            picked = jnp.stack([coarse[spread(x), spread(z)] for z in range(1, zs - 1)])
            s[f"v{level}a"][x, pl.ds(1, zs - 2)] = s[f"v{level}b"][x, pl.ds(1, zs - 2)] + picked
            return carry

        loop(xs - 2, add)
        held_sweep(level, s[f"v{level}a"], s[f"v{level}b"], 2)
        held_sweep(level, s[f"v{level}b"], out, 3, into=1)

    def own_of(level, ref):
        reach = REACH[level]
        xs, zs = ref.shape[:2]
        return ref[pl.ds(reach, xs - 2 * reach), pl.ds(reach, zs - 2 * reach)]

    def coefficients(level, kappa):
        coupling = 6.0 * 0.25**level
        s[f"d{level}"][...] = own_of(level, kappa) + coupling

        def body(x, carry):
            k = kappa[x]
            s[f"w{level}"][x] = jnp.where(k > 0.0, 0.8 / (k + coupling), 0.0)
            return carry

        loop(kappa.shape[0], body)

    def plane_copies(ref, sems, o):
        at = ref.at[me["gx"], me["gz"]]
        return pltpu.make_async_remote_copy(
            src_ref=at,
            dst_ref=at,
            send_sem=s["gsend"].at[sems, o],
            recv_sem=s["grecv"].at[sems, o],
            device_id=plane_peer(o),
            device_id_type=MESH,
        )

    def plane_start(ref, sems):
        def body(o, carry):
            plane_copies(ref, sems, o + 1).start()
            return carry

        loop(nx * nz - 1, body)

    def plane_finish(ref, sems):
        def body(o, carry):
            plane_copies(ref, sems, o + 1).wait_recv()
            return carry

        loop(nx * nz - 1, body)

        def body_send(o, carry):
            plane_copies(ref, sems, o + 1).wait_send()
            return carry

        loop(nx * nz - 1, body_send)

    def gather_start(n, field):
        pairs = pair_sum(field)
        s["g3"][n, me["gx"], me["gz"]] = moved(pairs[0, 0], "c230") + moved(pairs[1, 0], "c231")
        plane_start(s["g3"].at[n], n)

    def gather_finish(n):
        plane_finish(s["g3"].at[n], n)

    def coarsest(n):
        coupling = 0.25**LEVELS
        va, vb = s["gva"], s["gvb"]
        va[pl.ds(1, nx), pl.ds(1, nz)] = s["gw"][...] * s["g3"][n]
        glane, grow = lanes_of((nz, 8, LANES)), rows_of((nz, 8, LANES))
        inner = pl.ds(1, nz)

        def sweep(src, dst):
            def body(x, carry):
                here = src[x + 1, inner]
                along_x = turn(
                    here + jnp.where(glane >= 64, src[x, inner], src[x + 2, inner]), 64
                )
                along_z = swap_halves(
                    here
                    + jnp.where(grow >= HALF, src[x + 1, pl.ds(0, nz)], src[x + 1, pl.ds(2, nz)])
                )
                around = (along_x + along_z) + (turn(here, 1) + turn(here, LANES - 1))
                dst[x + 1, inner] = 0.2 * here + s["gw"][x] * (s["g3"][n, x] + coupling * around)
                return carry

            loop(nx, body, 0, 4)

        for i in range(COARSE_SWEEPS - 1):
            sweep(*((va, vb) if i % 2 == 0 else (vb, va)))
        done = vb if (COARSE_SWEEPS - 1) % 2 else va
        low_rows = rows_of((8, LANES)) < HALF
        near_me = []
        for i in range(3):
            below, mine, above = (done[i + me["gx"], j + me["gz"]] for j in range(3))
            near_me += [
                below,
                swap_halves(jnp.where(low_rows, mine, below)),
                mine,
                swap_halves(jnp.where(low_rows, above, mine)),
                above,
            ]
        near_me = jnp.stack(near_me)
        for i in range(2):
            spread = moved(near_me, f"p32{i}")
            for x in range(3):
                s["e3"][2 * x + i] = spread[5 * x : 5 * x + 5]

    def sum_start(dots, n):
        packed = jnp.zeros((8, LANES), F32)
        for j, d in enumerate(dots):
            packed = jnp.where(lane == j, jnp.sum(d, axis=-1, keepdims=True), packed)
        s["a1"][n, me["gx"], me["gz"]] = packed + swap_halves(packed)
        plane_start(s["a1"].at[n], 3 + n)

    def gy_copies(n):
        at = s["a2"].at[n, me["gy"]]
        return [
            pltpu.make_async_remote_copy(
                src_ref=at,
                dst_ref=at,
                send_sem=s["gsend"].at[5 + n, o],
                recv_sem=s["grecv"].at[5 + n, o],
                device_id={"gy": lax.rem(me["gy"] + o, counts["gy"])},
                device_id_type=MESH,
            )
            for o in range(1, counts["gy"])
        ]

    def folded(value):
        while value.shape[0] > 1:
            value = value[: value.shape[0] // 2] + value[value.shape[0] // 2 :]
        return value[0]

    def sum_middle(n):
        plane_finish(s["a1"].at[n], 3 + n)
        s["a2"][n, me["gy"]] = folded(s["a1"][n].reshape(nx * nz, 8, LANES))
        for c in gy_copies(n):
            c.start()

    def sum_finish(n, count):
        for c in gy_copies(n):
            c.wait_recv()
        for c in gy_copies(n):
            c.wait_send()
        total = folded(s["a2"][n])
        return [total[:, j : j + 1] for j in range(count)]

    kappa_1 = moved(s["t1"][...], "c01")
    kappa_2 = moved(pair_sum(kappa_1), "c12")
    pl.semaphore_wait(barrier, greeted)
    kappa_plans = {1: start_exchange(1, 0, kappa_1), 2: start_exchange(2, 0, kappa_2)}

    def cycle(n, meanwhile_1, meanwhile_2):
        put("a", lambda x: s["w0"][x] * s["b0"][x])
        put("b", swept("a"))

        def remainder(x):
            here, around = neighbours("b", x)
            return s["b0"][x] - (s["d0"][x] * here - around)

        def body(x, carry):
            s["t1"][x] = pair_sum(jnp.stack([remainder(2 * x), remainder(2 * x + 1)]))[0]
            return carry

        loop(8, body)
        plan = start_exchange(1, n, moved(s["t1"][...], "c01"))
        meanwhile_1()
        finish_exchange(1, n, plan, s["b1"])
        plan = start_exchange(2, n, moved(pair_sum(held_down(1)), "c12"))
        meanwhile_2()
        finish_exchange(2, n, plan, s["b2"])
        gather_start(n, held_down(2))
        if n == 1:
            gather_finish(0)
            kappa_3 = s["g3"][0]
            s["gw"][...] = jnp.where(kappa_3 > 0.0, 0.8 / (kappa_3 + 6.0 * 0.25**LEVELS), 0.0)
        gather_finish(n)
        coarsest(n)
        held_up(2, s["e3"], lambda i: i // 2, s["e2"], 3)
        s["t2"][...] = moved(s["e2"][...], "p21")
        held_up(1, s["t2"], lambda i: (i - 1) // 2, s["e1"], 3)
        s["t1"][...] = moved(s["e1"][...], "p10")

        def corrected(x):
            e = s["t1"][x // 2]
            return s["v0b"][x + 1, pl.ds(1, 8)] + jnp.stack([e, e], axis=1).reshape(8, 8, LANES)

        put("a", corrected)
        put("b", swept("a"))
        put("c", swept("b"))

        def apply(x, c):
            here, around = neighbours("c", x)
            q = s["d0"][x] * here - around
            s["z"][n - 1, x] = here
            s["q"][n - 1, x] = q
            b = s["b0"][x]
            if n == 1:
                s["flip"][x] = b.reshape(64, LANES)
                s["b0"][x] = q
            return c[0] + folded(b * here), c[1] + folded(here * q)

        return loop(16, apply, (jnp.zeros((8, LANES), F32),) * 2)

    def kappa_held_1():
        finish_exchange(1, 0, kappa_plans[1], s["v1a"])
        coefficients(1, s["v1a"])
        finish_exchange(2, 0, kappa_plans[2], s["v2a"])
        coefficients(2, s["v2a"])
        gather_start(0, own_of(2, s["v2a"]))

    sum_start(cycle(1, kappa_held_1, lambda: None), 0)
    cycle(2, lambda: sum_middle(0), lambda: None)
    rz, zq = sum_finish(0, 2)
    step = jnp.broadcast_to(rz / zq, (8, LANES))
    zero = jnp.zeros((8, LANES), F32)

    def dots_second(x, c):
        q0 = s["q"][0, x]
        z0 = s["z"][0, x]
        r1 = s["flip"][x].reshape(8, 8, LANES) - step * q0
        z1 = z0 - step * s["z"][1, x]
        q1 = q0 - step * s["q"][1, x]
        s["z"][1, x] = z1
        pairs = (
            (r1, z1),
            (z1, q1),
            (z1, q0),
            (z0, q1),
            (r1, r1),
            (r1, q1),
            (r1, q0),
            (q1, q1),
            (q1, q0),
            (q0, q0),
        )
        return tuple(t + folded(u * v) for t, (u, v) in zip(c, pairs))

    sum_start(loop(16, dots_second, (zero,) * 10), 1)
    sum_middle(1)
    r1z1, z1q1, z1q0, z0q1, r1r1, r1q1, r1q0, q1q1, q1q0, q0q0 = sum_finish(1, 10)
    ratio = r1z1 / rz
    step2 = r1z1 / (z1q1 + ratio * (z1q0 + z0q1) + ratio * ratio * zq)
    squares = (
        r1r1
        - 2.0 * step2 * (r1q1 + ratio * r1q0)
        + step2 * step2 * (q1q1 + 2.0 * ratio * q1q0 + ratio * ratio * q0q0)
    )
    norm = jnp.sqrt(jnp.maximum(squares, 0.0) * (1.0 / cells))
    norm_ref[...] = jnp.broadcast_to(norm, (8, LANES))
    along_z0 = jnp.broadcast_to(step + step2 * ratio, (8, LANES))
    along_z1 = jnp.broadcast_to(step2, (8, LANES))

    def finish(x, c):
        value = along_z0 * s["z"][0, x] + along_z1 * s["z"][1, x]
        s["flip"][x] = value.reshape(64, LANES)
        return c

    loop(16, finish)

    def write(x, c):
        for p in range(PROBES):
            for h in range(2):
                row = h * PROBES + p
                solution_ref[p, x, pl.ds(8 * h, 8), :] = s["flip"][x, pl.ds(row, 8, stride=8), :]
        return c

    loop(16, write)


MATRICES = ("c01", "c12", "p10", "p21", "c230", "c231", "p320", "p321")


def scratch_list():
    def fields(*lead):
        return pltpu.VMEM((*lead, 8, LANES), F32)

    out = {"flip": pltpu.VMEM((16, 64, LANES), F32), "lanes": pltpu.VMEM((8, LANES, LANES), F32)}
    for name in ("b0", "d0", "w0"):
        out[name] = fields(16, 8)
    for which in "abc":
        out[f"v0{which}"] = fields(18, 10)
        out[f"r0{which}"] = fields(2, 8)
        out[f"p0{which}"] = fields(2, 8)
        out[f"r0{which}y"] = fields(2)
        out[f"p0{which}y"] = fields(2)
    for level, xs, zs in ((1, 8, 4), (2, 4, 2)):
        reach = REACH[level]
        for name in (f"b{level}", f"w{level}", f"v{level}a", f"v{level}b"):
            out[name] = fields(xs + 2 * reach, zs + 2 * reach)
        out[f"d{level}"] = fields(xs, zs)
    out["e1"] = fields(8, 4)
    out["t1"] = fields(8, 4)
    out["e2"] = fields(6, 4)
    out["t2"] = fields(6, 4)
    out["e3"] = fields(6, 5)
    out["m1"] = fields(3, 3, 3, 4, 4)
    out["y1"] = fields(3, 3, 3, 2)
    out["y1out"] = fields(3, 2)
    out["m2"] = fields(3, 3, 3, 3, 2)
    out["z"] = fields(2, 16, 8)
    out["q"] = fields(2, 16, 8)
    out["g3"] = fields(3, 8, 4)
    out["a1"] = fields(2, 8, 4)
    out["a2"] = fields(2, 4)
    out["gw"] = fields(8, 4)
    out["gva"] = fields(10, 6)
    out["gvb"] = fields(10, 6)
    out["send"] = pltpu.SemaphoreType.DMA((3, 6))
    out["recv"] = pltpu.SemaphoreType.DMA((3, 6))
    out["xsend"] = pltpu.SemaphoreType.DMA((2, 3, 27))
    out["xrecv"] = pltpu.SemaphoreType.DMA((2, 3, 27))
    out["gsend"] = pltpu.SemaphoreType.DMA((7, 32))
    out["grecv"] = pltpu.SemaphoreType.DMA((7, 32))
    return out


def solution(mesh):
    counts = {a: mesh.shape[a] for a in ("gx", "gy", "gz")}

    def step(kappa_sq, probe_bits):
        cells = probe_bits[0].size * counts["gx"] * counts["gy"] * counts["gz"]
        whole, norms = pl.pallas_call(
            functools.partial(kernel_body, counts, cells),
            out_shape=(
                jax.ShapeDtypeStruct(probe_bits.shape, F32),
                jax.ShapeDtypeStruct((8, LANES), F32),
            ),
            in_specs=[pl.BlockSpec(memory_space=pltpu.VMEM)] * 2,
            out_specs=(pl.BlockSpec(memory_space=pltpu.VMEM),) * 2,
            scratch_shapes=list(scratch_list().values()),
            compiler_params=pltpu.CompilerParams(
                collective_id=0, has_side_effects=True, vmem_limit_bytes=40 * 2**20
            ),
            name="solve",
        )(kappa_sq, probe_bits)
        return whole, norms[:PROBES, 0]

    return jax.shard_map(
        step,
        mesh=mesh,
        in_specs=(P("gx", "gz", "gy"), P(None, "gx", "gz", "gy")),
        out_specs=(P(None, "gx", "gz", "gy"), P()),
        check_vma=False,
    )
```

time: 175 us -> 131 us (0.75)
  Pallas kernels: 170 us -> 127 us
    pallas_call x1, Pallas kernels: 170 us -> 127 us  [step(): pl.pallas_call(functools.partial(kernel_body, counts, cells), out_shape=(...]
where the time goes in v2:
time: 131 us
  Pallas kernels  127 us (97%)
  local copies, waits for them, and re-layouts  3.36 us (3%)
    pallas_call x1, Pallas kernels, step(): pl.pallas_call(functools.partial(kernel_body, counts, cells), out_shape=(...  127 us
    unnamed x5, local copies, waits for them, and re-layouts  2.73 us

profile of v2, /device:TPU:0, one launch (start us, length us, event | category | flops | bytes accessed | tf_op | source)
XLA Modules:
  0.0 130.8 jit_solution(15379687058029140592)
XLA Ops:
  0.6 0.0 copy-start
  0.6 1.0 copy-done
  1.7 0.0 copy-start.1
  1.7 0.9 copy-done.1
  2.6 126.8 %solve.1 = (f32[4,16,16,128]{3,2,1,0:T(8,128)S(1)}, f32[8,128]{1,0:T(8,128)S(1)}) custom-call(f32[16,16,128]{2,1,0:T(8,128)S(1)} %copy-done.1, s32[4,16,16,128]{3,2,1,0:T(8,128)S(1)} %copy-done), custom_call_target="tpu_custom_call" | custom-call | tf_op jit(solution)/shard_map/solve/pallas_call | solution.py:753
  129.4 0.6 slice_reduce_fusion
  130.0 0.8 copy.5
Async XLA Ops:
  0.6 1.0 copy-start
  1.7 0.9 copy-start.1

commit v3 on v2

v3 whole, which is shorter than its diff:
```python
import functools

import jax
import jax.numpy as jnp
from jax import lax
from jax.experimental import pallas as pl
from jax.experimental.pallas import tpu as pltpu
from jax.sharding import PartitionSpec as P

LEVELS = 3
COARSE_SWEEPS = 8
PROBES = 4
LANES = 128
HALF = 4
MESH = pl.DeviceIdType.MESH
F32 = jnp.float32

OWN = {1: 32, 2: 48, 3: 24}
REACH = {1: 3, 2: 4}
HELD = {1: (14, 10), 2: (12, 10)}
CORE = {1: (8, 4), 2: (4, 2)}


def lanes_of(shape):
    return lax.broadcasted_iota(jnp.int32, shape, len(shape) - 1)


def rows_of(shape):
    return lax.broadcasted_iota(jnp.int32, shape, len(shape) - 2)


def turn(value, shift):
    return pltpu.roll(value, shift, len(value.shape) - 1)


def swap_halves(value):
    return pltpu.roll(value, HALF, len(value.shape) - 2)


def kernel_body(counts, cells, kappa_ref, bits_ref, solution_ref, norm_ref, *scratch):
    s = dict(zip(scratch_list(), scratch))
    axes = ("gx", "gz", "gy")
    me = {a: lax.axis_index(a) for a in axes}
    nx, nz = counts["gx"], counts["gz"]
    lane = lanes_of((8, LANES))

    def loop(count, body, init=0, unroll=1):
        return lax.fori_loop(0, count, body, init, unroll=count)

    def exists(steps):
        ok = None
        for a, d in zip(axes, steps):
            if d:
                one = me[a] > 0 if d < 0 else me[a] < counts[a] - 1
                ok = one if ok is None else ok & one
        return ok

    def device(steps):
        return {a: me[a] + d for a, d in zip(axes, steps)}

    around_me = [
        (i, j, k) for i in (-1, 0, 1) for j in (-1, 0, 1) for k in (-1, 0, 1) if (i, j, k) != (0, 0, 0)
    ]

    def clear_faces(i, carry):
        for x in (0, 17):
            s["v0"][i, x] = jnp.zeros(s["v0"].shape[2:], F32)
        for name in ("r0", "r0y"):
            s[name][i] = jnp.zeros(s[name].shape[1:], F32)
        return carry

    loop(3, clear_faces)
    for name in ("m1", "y1", "m2"):
        ref = s[name]

        def clear(i, carry, ref=ref):
            for j in range(3):
                ref[i // 3, lax.rem(i, 3), j] = jnp.zeros(ref.shape[3:], F32)
            return carry

        loop(9, clear)

    def clear_coarse(i, carry):
        s["gv"][i // 10, lax.rem(i, 10)] = jnp.zeros(s["gv"].shape[2:], F32)
        return carry

    loop(20, clear_coarse)

    barrier = pltpu.get_barrier_semaphore()

    def greet(to):
        pl.semaphore_signal(barrier, inc=1, device_id=to, device_id_type=MESH)

    def wrapped(a, step):
        to = me[a] + step
        return jnp.where(to >= counts[a], to - counts[a], to)

    def plane_peer(i, j):
        return {"gx": wrapped("gx", i), "gz": wrapped("gz", j)}

    plane_offsets = sorted(
        ((i, j) for i in range(nx) for j in range(nz) if (i, j) != (0, 0)),
        key=lambda at: -min(at[0], nx - at[0]) - 2 * min(at[1], nz - at[1]),
    )
    for i, j in plane_offsets:
        greet(plane_peer(i, j))
    for o in range(1, counts["gy"]):
        greet({"gy": lax.rem(me["gy"] + o, counts["gy"])})
    for steps in around_me:
        if steps[2] and steps[:2] != (0, 0):
            pl.when(exists(steps))(functools.partial(greet, device(steps)))
    near = {
        a: (me[a] > 0).astype(jnp.int32) + (me[a] < counts[a] - 1).astype(jnp.int32) for a in axes
    }
    greeted = (
        nx * nz - 1 + counts["gy"] - 1 + ((near["gx"] + 1) * (near["gz"] + 1) - 1) * near["gy"]
    )

    row_at = rows_of((LANES, LANES))
    col_at = lanes_of((LANES, LANES))

    def halved(value):
        return (value + 256) // 2 - 128

    def keep(name, where, weight):
        s["lanes"][MATRICES.index(name)] = jnp.where(where, weight, 0.0).astype(jnp.bfloat16)

    keep("c01", col_at == 32 + row_at // 2, 0.125)
    keep("c12", (col_at == 48 + halved(row_at - 32)) & (row_at >= 32) & (row_at < 96), 0.125)
    inside = (row_at >= 18) & (row_at < 110)
    keep("p10", row_at == 32 + col_at // 2, 1.0)
    keep("p21", row_at == 48 + halved(col_at - 32), 1.0)
    for i in range(2):
        keep(f"c23{i}", (col_at == 64 * i + 24 + halved(row_at - 48)) & inside, 0.125)
        keep(f"p32{i}", row_at == 64 * i + 24 + halved(col_at - 48), 1.0)

    def moved(value, name):
        shape = value.shape
        rest = value.reshape(-1, LANES)
        matrix = s["lanes"][MATRICES.index(name)]
        total = None
        for _ in range(3):
            part = rest.astype(jnp.bfloat16)
            rest = rest - part.astype(F32)
            product = jnp.dot(part, matrix, preferred_element_type=F32)
            total = product if total is None else total + product
        return total.reshape(shape)

    def moved_rows(source, target, name, rows):
        def body(i, carry):
            at = pl.ds(i * rows, rows)
            target[at] = moved(source[at], name)
            return carry

        loop(source.shape[0] // rows, body)

    def load_x(x, carry):
        for p in range(PROBES):
            for h in range(2):
                row = h * PROBES + p
                s["flip"][x, pl.ds(row, 8, stride=8), :] = (
                    2.0 * bits_ref[p, x, pl.ds(8 * h, 8), :].astype(F32) - 1.0
                )
        return carry

    def take_x(x, carry):
        s["b0"][x] = s["flip"][x].reshape(8, 8, LANES)
        return carry

    def kappa_x(x, carry):
        for p in range(PROBES):
            for h in range(2):
                row = h * PROBES + p
                s["flip"][x, pl.ds(row, 8, stride=8), :] = kappa_ref[x, pl.ds(8 * h, 8), :]
        return carry

    def pair_sum(field):
        xs, zs = field.shape[0] // 2, field.shape[1] // 2
        split = field.reshape(xs, 2, zs, 2, 8, LANES)
        return (split[:, 0, :, 0] + split[:, 0, :, 1]) + (split[:, 1, :, 0] + split[:, 1, :, 1])

    def diag_x(x, carry):
        kappas = [s["flip"][2 * x + i].reshape(8, 8, LANES) for i in range(2)]
        for i in range(2):
            s["d0"][2 * x + i] = kappas[i] + 6.0
            s["w0"][2 * x + i] = 0.8 / (kappas[i] + 6.0)
        s["t1"][x] = pair_sum(jnp.stack(kappas))[0]
        return carry

    loop(16, load_x)
    loop(16, take_x)
    loop(16, kappa_x)
    loop(8, diag_x)

    def wait_for(count, send, recv):
        ref = s["count"].at[pl.ds(0, count)]
        c = pltpu.make_async_remote_copy(
            src_ref=ref,
            dst_ref=ref,
            send_sem=send,
            recv_sem=recv,
            device_id={"gx": lax.rem(me["gx"] + 1, nx)},
            device_id_type=MESH,
        )
        c.wait_recv()
        c.wait_send()

    def wait_near(count_of, send, recv):
        for x in (1, 2):
            for z in (1, 2):
                for y in (1, 2):
                    here = (near["gx"] == x) & (near["gz"] == z) & (near["gy"] == y)
                    pl.when(here)(functools.partial(wait_for, count_of(x, z, y), send, recv))

    def exchange(which):
        v = s["v0"].at[which]
        got = s["r0"].at[which]
        pack = s["p0"].at[which]
        yin = s["r0y"].at[which]
        yout = s["p0y"].at[which]
        low_rows = rows_of((8, LANES)) < HALF

        def pack_z(x, carry):
            pack[0, x] = jnp.where(low_rows, v[x + 1, 1], swap_halves(v[x + 9, 1]))
            pack[1, x] = jnp.where(low_rows, swap_halves(v[x + 1, 8]), v[x + 9, 8])
            return carry

        loop(8, pack_z, 0, 4)

        group = ((lane + 1) & (LANES - 1)) // 16

        def pack_y(x, carry):
            low, high = carry
            ends = v[x + 1, 1]
            for z in range(1, 8):
                ends = jnp.where(group == z, turn(v[x + 1, 1 + z], 16 * z), ends)
            ends = turn(ends, x)
            low = jnp.where((lane & 15) == x, ends, low)
            high = jnp.where((lane & 15) == ((x + 15) & 15), ends, high)
            return low, high

        zero = jnp.zeros((8, LANES), F32)
        yout[0], yout[1] = loop(16, pack_y, (zero, zero), 8)
        inner = pl.ds(1, 8)
        for steps, src, dst in (
            ((0, -1, 0), pack.at[0], got.at[1]),
            ((0, 1, 0), pack.at[1], got.at[0]),
            ((-1, 0, 0), v.at[1, inner], v.at[17, inner]),
            ((1, 0, 0), v.at[16, inner], v.at[0, inner]),
            ((0, 0, -1), yout.at[0], yin.at[1]),
            ((0, 0, 1), yout.at[1], yin.at[0]),
        ):
            c = pltpu.make_async_remote_copy(
                src_ref=src,
                dst_ref=dst,
                send_sem=s["send"].at[which],
                recv_sem=s["recv"].at[which],
                device_id=device(steps),
                device_id_type=MESH,
            )
            pl.when(exists(steps))(c.start)
        wait_near(lambda x, z, y: 8 * (x + z) + y, s["send"].at[which], s["recv"].at[which])

        def unpack_z(x, carry):
            low, high = got[0, x], got[1, x]
            v[x + 1, 0] = jnp.where(low_rows, low, swap_halves(v[x + 1, 8]))
            v[x + 9, 0] = swap_halves(jnp.where(low_rows, v[x + 9, 8], low))
            v[x + 1, 9] = swap_halves(jnp.where(low_rows, high, v[x + 1, 1]))
            v[x + 9, 9] = jnp.where(low_rows, swap_halves(v[x + 9, 1]), high)
            return carry

        loop(8, unpack_z, 0, 4)

        def unpack_y(x, carry):
            before = turn(yin[0], (LANES + 1 - x) & (LANES - 1))
            after = turn(yin[1], LANES - 1 - x)
            s["ends"][x, 0] = jnp.where((lane & 15) == 0, before, after)
            return carry

        loop(16, unpack_y, 0, 8)

    def neighbours(which, x):
        v = s["v0"].at[which]
        here = v[x + 1, pl.ds(1, 8)]
        total = v[x, pl.ds(1, 8)] + v[x + 2, pl.ds(1, 8)]
        total = total + (v[x + 1, pl.ds(0, 8)] + v[x + 1, pl.ds(2, 8)])
        ends = s["ends"][x, 0]
        ends = jnp.stack([ends] + [turn(ends, LANES - 16 * z) for z in range(1, 8)])
        at_lane = lanes_of((8, 8, LANES))
        before = jnp.where(at_lane == 0, ends, turn(here, 1))
        after = jnp.where(at_lane == LANES - 1, ends, turn(here, LANES - 1))
        return here, total + (before + after)

    def put(which, row, unroll):
        def body(x, carry):
            s["v0"][which, x + 1, pl.ds(1, 8)] = row(x)
            return carry

        loop(16, body, 0, unroll)

    def sweep(which, into):
        def row(x):
            here, around = neighbours(which, x)
            return 0.2 * here + s["w0"][x] * (s["b0"][x] + around)

        put(into, row, 4)

    def start_exchange(level, n, field):
        if level == 1:

            def pack_x(i, carry):
                s["m1"][n, 1, 1, i] = turn(field[2 * i], LANES - 32) + turn(field[2 * i + 1], 32)
                return carry

            loop(4, pack_x, 0, 2)

            def pack_y(x, carry):
                low, high = carry
                for z in range(4):
                    at = 16 * x + 4 * z
                    slot = (lane >> 2) == 4 * x + z
                    value = field[x, z]
                    low = jnp.where(slot, turn(value, (at + LANES - 32) & (LANES - 1)), low)
                    high = jnp.where(slot, turn(value, (at + LANES - 92) & (LANES - 1)), high)
                return low, high

            zero = jnp.zeros((8, LANES), F32)
            low, high = loop(8, pack_y, (zero, zero), 2)
            s["y1out"][n, 0] = high
            s["y1out"][n, 1] = low
        else:
            both = pl.ds(0, 2)
            total = turn(field[0, both], LANES - 48)
            for x in range(1, 4):
                total = total + turn(field[x, both], (32 * x + LANES - 48) % LANES)
            s["m2"][n, 1, 1, 1, both] = total
        for steps in around_me:
            i, j, k = steps
            if level == 2:
                src = s["m2"].at[n, 1, 1, 1, pl.ds(0, 2)]
                dst = s["m2"].at[n, 1 - i, 1 - j, 1 - k, pl.ds(0, 2)]
            elif k:
                side = 0 if k > 0 else 1
                src = s["y1out"].at[n, side]
                dst = s["y1"].at[n, 1 - i, 1 - j, side]
            else:
                if j == 0:
                    part = (pl.ds(0 if i < 0 else 2, 2),)
                elif i == 0:
                    part = (slice(None), pl.ds(0 if j < 0 else 1, 3))
                else:
                    part = (pl.ds(0 if i < 0 else 3, 1), pl.ds(0 if j < 0 else 2, 2))
                src = s["m1"].at[(n, 1, 1, *part)]
                dst = s["m1"].at[(n, 1 - i, 1 - j, *part)]
            c = pltpu.make_async_remote_copy(
                src_ref=src,
                dst_ref=dst,
                send_sem=s["xsend"].at[level - 1, n],
                recv_sem=s["xrecv"].at[level - 1, n],
                device_id=device(steps),
                device_id_type=MESH,
            )
            pl.when(exists(steps))(c.start)

    def finish_exchange(level, n, out):
        def count_of(x, z, y):
            if level == 2:
                return 2 * ((x + 1) * (z + 1) * (y + 1) - 1)
            return 8 * x + 12 * z + 2 * x * z + (x + 1) * (z + 1) * y

        wait_near(count_of, s["xsend"].at[level - 1, n], s["xrecv"].at[level - 1, n])
        low_rows = rows_of((8, LANES)) < HALF
        reach = REACH[level]
        xs, zs = (8, 4) if level == 1 else (4, 2)

        def body(x, carry):
            far = (x + xs - reach) // xs
            at_x = lax.rem(x + xs - reach, xs)

            def source(j, z):
                if level == 1:
                    mid = turn(
                        s["m1"][n, far, j, at_x // 2, z], 32 + 64 * lax.rem(at_x, 2)
                    )
                    at = 4 * (4 * at_x + z)
                    left = turn(s["y1"][n, far, j, 0], lax.rem(28 - at + 2 * LANES, LANES))
                    right = turn(s["y1"][n, far, j, 1], lax.rem(96 - at + 2 * LANES, LANES))
                    value = jnp.where((lane >= 28) & (lane < 32), left, 0.0)
                    value = jnp.where((lane >= 96) & (lane < 100), right, value)
                    return jnp.where((lane >= 32) & (lane < 96), mid, value)
                value = jnp.zeros((8, LANES), F32)
                for k in range(3):
                    start = 16 + 32 * k
                    part = turn(
                        s["m2"][n, far, j, k, z], lax.rem(start + 2 * LANES - 32 * at_x, LANES)
                    )
                    value = jnp.where((lane >= start) & (lane < start + 32), part, value)
                return value

            mine = [source(1, z) for z in range(zs)]
            if level == 1:
                down = [None] + [source(0, z) for z in (1, 2, 3)]
                over = [source(2, z) for z in (0, 1, 2)]
                below = [(down[z], mine[z]) for z in (1, 2, 3)]
                above = [(over[z], mine[z]) for z in (0, 1, 2)]
                outer_low, outer_high = [], []
            else:
                outer_low = [source(0, z) for z in range(2)]
                outer_high = [source(2, z) for z in range(2)]
                below = list(zip(outer_low, mine))
                above = list(zip(outer_high, mine))
            values = list(outer_low)
            values += [swap_halves(jnp.where(low_rows, own, other)) for other, own in below]
            values += mine
            values += [swap_halves(jnp.where(low_rows, other, own)) for other, own in above]
            values += outer_high
            out[x, pl.ds(0, len(values))] = jnp.stack(values)
            return carry

        loop(xs + 2 * reach, body, 0, 2)

    def held_row(src, x, z0, z1):
        inner = pl.ds(z0, z1 - z0)
        here = src[x, inner]
        total = (src[x - 1, inner] + src[x + 1, inner]) + (
            src[x, pl.ds(z0 - 1, z1 - z0)] + src[x, pl.ds(z0 + 1, z1 - z0)]
        )
        return here, total + (turn(here, 1) + turn(here, LANES - 1))

    def held_sweep(level, src, dst, margin, into=0):
        xs, zs = HELD[level]
        coupling = 0.25**level
        z0, z1 = margin, zs - margin

        def body(i, carry):
            x = i + margin
            here, around = held_row(src, x, z0, z1)
            inner = pl.ds(z0, z1 - z0)
            value = 0.2 * here + s[f"w{level}"][x, inner] * (
                s[f"b{level}"][x, inner] + coupling * around
            )
            if into:
                dst[i] = value
            else:
                dst[x, inner] = value
            return carry

        loop(xs - 2 * margin, body, 0, 2)

    def held_down(level):
        xs, zs = HELD[level]
        reach = REACH[level]
        coupling = 0.25**level

        def begin(x, carry):
            s[f"v{level}a"][x] = s[f"w{level}"][x] * s[f"b{level}"][x]
            return carry

        loop(xs, begin)
        held_sweep(level, s[f"v{level}a"], s[f"v{level}b"], 1)
        z0, z1 = reach, zs - reach
        inner = pl.ds(z0, z1 - z0)

        def remainder(x):
            here, around = held_row(s[f"v{level}b"], x + reach, z0, z1)
            return s[f"b{level}"][x + reach, inner] - (
                s[f"d{level}"][x, pl.ds(0, CORE[level][1])] * here - coupling * around
            )

        def body(x, carry):
            pair = pair_sum(jnp.stack([remainder(2 * x), remainder(2 * x + 1)]))[0]
            s[f"f{level + 1}"][x, pl.ds(0, CORE[level][1] // 2)] = pair
            return carry

        loop((xs - 2 * reach) // 2, body, 0, 2)

    def held_up(level, coarse, spread, out, last_margin):
        xs, zs = HELD[level]

        def add(i, carry):
            x = i + 1
            picked = jnp.stack([coarse[spread(x), spread(z)] for z in range(1, zs - 1)])
            s[f"v{level}a"][x, pl.ds(1, zs - 2)] = s[f"v{level}b"][x, pl.ds(1, zs - 2)] + picked
            return carry

        loop(xs - 2, add)
        held_sweep(level, s[f"v{level}a"], s[f"v{level}b"], 2)
        held_sweep(level, s[f"v{level}b"], out, 3, into=1)

    def own_of(level, ref):
        reach = REACH[level]
        xs, zs = HELD[level]
        return ref[pl.ds(reach, xs - 2 * reach), pl.ds(reach, zs - 2 * reach)]

    def coefficients(level, kappa):
        coupling = 6.0 * 0.25**level
        s[f"d{level}"][:, pl.ds(0, CORE[level][1])] = own_of(level, kappa) + coupling

        def body(x, carry):
            k = kappa[x]
            s[f"w{level}"][x] = jnp.where(k > 0.0, 0.8 / (k + coupling), 0.0)
            return carry

        loop(kappa.shape[0], body)

    def plane_start(ref, sems):
        at = ref.at[me["gx"], me["gz"]]
        for i, j in plane_offsets:
            pltpu.make_async_remote_copy(
                src_ref=at,
                dst_ref=at,
                send_sem=s["gsend"].at[sems],
                recv_sem=s["grecv"].at[sems],
                device_id=plane_peer(i, j),
                device_id_type=MESH,
            ).start()

    def plane_finish(sems):
        wait_for(nx * nz - 1, s["gsend"].at[sems], s["grecv"].at[sems])

    def gather_start(n):
        s["g3"][n, me["gx"], me["gz"]] = moved(s["f3"][0, 0], "c230") + moved(s["f3"][1, 0], "c231")
        plane_start(s["g3"].at[n], n)

    def gather_finish(n):
        plane_finish(n)

    def coarsest(n):
        coupling = 0.25**LEVELS
        inner = pl.ds(1, nz)
        s["gv"][0, pl.ds(1, nx), inner] = s["gw"][...] * s["g3"][n]
        glane, grow = lanes_of((nz, 8, LANES)), rows_of((nz, 8, LANES))

        def coarse_sweep(src, dst):
            def body(x, carry):
                here = src[x + 1, inner]
                along_x = turn(
                    here + jnp.where(glane >= 64, src[x, inner], src[x + 2, inner]), 64
                )
                along_z = swap_halves(
                    here
                    + jnp.where(grow >= HALF, src[x + 1, pl.ds(0, nz)], src[x + 1, pl.ds(2, nz)])
                )
                around = (along_x + along_z) + (turn(here, 1) + turn(here, LANES - 1))
                dst[x + 1, inner] = 0.2 * here + s["gw"][x] * (s["g3"][n, x] + coupling * around)
                return carry

            loop(nx, body, 0, nx)

        for i in range(COARSE_SWEEPS - 1):
            coarse_sweep(s["gv"].at[i % 2], s["gv"].at[1 - i % 2])
        done = s["gv"].at[(COARSE_SWEEPS - 1) % 2]
        low_rows = rows_of((8, LANES)) < HALF
        near_me = []
        for i in range(3):
            below, mine, above = (done[i + me["gx"], j + me["gz"]] for j in range(3))
            near_me += [
                below,
                swap_halves(jnp.where(low_rows, mine, below)),
                mine,
                swap_halves(jnp.where(low_rows, above, mine)),
                above,
            ]
        near_me = jnp.stack(near_me)
        for i in range(2):
            spread = moved(near_me, f"p32{i}")
            for x in range(3):
                s["e3"][2 * x + i, pl.ds(0, 5)] = spread[5 * x : 5 * x + 5]

    def sum_start(dots, n):
        packed = jnp.zeros((8, LANES), F32)
        for j, d in enumerate(dots):
            packed = jnp.where(lane == j, jnp.sum(d, axis=-1, keepdims=True), packed)
        s["a1"][n, me["gx"], me["gz"]] = packed + swap_halves(packed)
        plane_start(s["a1"].at[n], 3 + n)

    def folded(value):
        while value.shape[0] > 1:
            value = value[: value.shape[0] // 2] + value[value.shape[0] // 2 :]
        return value[0]

    def sum_middle(n):
        plane_finish(3 + n)
        s["a2"][n, me["gy"]] = folded(s["a1"][n].reshape(nx * nz, 8, LANES))
        at = s["a2"].at[n, me["gy"]]
        for o in range(1, counts["gy"]):
            pltpu.make_async_remote_copy(
                src_ref=at,
                dst_ref=at,
                send_sem=s["gsend"].at[5 + n],
                recv_sem=s["grecv"].at[5 + n],
                device_id={"gy": wrapped("gy", o)},
                device_id_type=MESH,
            ).start()

    def sum_finish(n, count):
        wait_for(counts["gy"] - 1, s["gsend"].at[5 + n], s["grecv"].at[5 + n])
        total = folded(s["a2"][n])
        return [total[:, j : j + 1] for j in range(count)]

    moved_rows(s["t1"], s["f1"], "c01", 4)

    def pair_up(x, carry):
        s["f2"][x, pl.ds(0, 2)] = pair_sum(s["f1"][pl.ds(2 * x, 2)])[0]
        return carry

    loop(4, pair_up)
    pl.semaphore_wait(barrier, greeted)
    start_exchange(1, 0, s["f1"])
    s["t3"][:, pl.ds(0, 2)] = moved(s["f2"][:, pl.ds(0, 2)], "c12")
    start_exchange(2, 0, s["t3"])

    def coefficients_held():
        finish_exchange(1, 0, s["v1a"])
        coefficients(1, s["v1a"])
        finish_exchange(2, 0, s["v2a"])
        coefficients(2, s["v2a"])
        s["f3"][:, pl.ds(0, 1)] = pair_sum(own_of(2, s["v2a"]))
        gather_start(0)

    def coarse_coefficients():
        gather_finish(0)
        kappa_3 = s["g3"][0]
        s["gw"][...] = jnp.where(kappa_3 > 0.0, 0.8 / (kappa_3 + 6.0 * 0.25**LEVELS), 0.0)

    def below(n):
        def remainder(x):
            here, around = neighbours(1, x)
            return s["b0"][x] - (s["d0"][x] * here - around)

        def body(x, carry):
            s["t1"][x] = pair_sum(jnp.stack([remainder(2 * x), remainder(2 * x + 1)]))[0]
            return carry

        loop(8, body, 0, 2)
        moved_rows(s["t1"], s["f1"], "c01", 4)
        start_exchange(1, n, s["f1"])
        pl.when(n == 1)(coefficients_held)
        pl.when(n == 2)(lambda: sum_middle(0))
        finish_exchange(1, n, s["b1"])
        held_down(1)
        s["t3"][:, pl.ds(0, 2)] = moved(s["f2"][:, pl.ds(0, 2)], "c12")
        start_exchange(2, n, s["t3"])
        finish_exchange(2, n, s["b2"])
        held_down(2)
        pl.when(n == 1)(coarse_coefficients)
        gather_start(n)
        gather_finish(n)
        coarsest(n)
        held_up(2, s["e3"], lambda i: i // 2, s["e2"], 3)
        moved_rows(s["e2"], s["t2"], "p21", 3)
        held_up(1, s["t2"], lambda i: (i - 1) // 2, s["e1"], 3)
        moved_rows(s["e1"], s["t1"], "p10", 4)

    def corrected(x):
        e = s["t1"][x // 2]
        return s["v0"][1, x + 1, pl.ds(1, 8)] + jnp.stack([e, e], axis=1).reshape(8, 8, LANES)

    def cycle(n, carry):
        put(0, lambda x: s["w0"][x] * s["b0"][x], 2)
        exchange(0)
        sweep(0, 1)
        exchange(1)
        below(n)
        put(0, corrected, 2)
        exchange(0)
        sweep(0, 1)
        exchange(1)
        sweep(1, 2)
        exchange(2)

        def apply(x, c):
            here, around = neighbours(2, x)
            q = s["d0"][x] * here - around
            s["z"][n - 1, x] = here
            s["q"][n - 1, x] = q
            b = s["b0"][x]

            @pl.when(n == 1)
            def _():
                s["flip"][x] = b.reshape(64, LANES)
                s["b0"][x] = q

            return c[0] + folded(b * here), c[1] + folded(here * q)

        dots = loop(16, apply, (jnp.zeros((8, LANES), F32),) * 2, 2)
        pl.when(n == 1)(lambda: sum_start(dots, 0))
        return carry

    lax.fori_loop(1, 3, cycle, 0)
    rz, zq = sum_finish(0, 2)
    step = jnp.broadcast_to(rz / zq, (8, LANES))
    zero = jnp.zeros((8, LANES), F32)

    def dots_second(x, c):
        q0 = s["q"][0, x]
        z0 = s["z"][0, x]
        r1 = s["flip"][x].reshape(8, 8, LANES) - step * q0
        z1 = z0 - step * s["z"][1, x]
        q1 = q0 - step * s["q"][1, x]
        s["z"][1, x] = z1
        pairs = (
            (r1, z1),
            (z1, q1),
            (z1, q0),
            (z0, q1),
            (r1, r1),
            (r1, q1),
            (r1, q0),
            (q1, q1),
            (q1, q0),
            (q0, q0),
        )
        return tuple(t + folded(u * v) for t, (u, v) in zip(c, pairs))

    sum_start(loop(16, dots_second, (zero,) * 10), 1)
    sum_middle(1)
    r1z1, z1q1, z1q0, z0q1, r1r1, r1q1, r1q0, q1q1, q1q0, q0q0 = sum_finish(1, 10)
    ratio = r1z1 / rz
    step2 = r1z1 / (z1q1 + ratio * (z1q0 + z0q1) + ratio * ratio * zq)
    squares = (
        r1r1
        - 2.0 * step2 * (r1q1 + ratio * r1q0)
        + step2 * step2 * (q1q1 + 2.0 * ratio * q1q0 + ratio * ratio * q0q0)
    )
    norm = jnp.sqrt(jnp.maximum(squares, 0.0) * (1.0 / cells))
    norm_ref[...] = jnp.broadcast_to(norm, (8, LANES))
    along_z0 = jnp.broadcast_to(step + step2 * ratio, (8, LANES))
    along_z1 = jnp.broadcast_to(step2, (8, LANES))

    def finish(x, c):
        value = along_z0 * s["z"][0, x] + along_z1 * s["z"][1, x]
        s["flip"][x] = value.reshape(64, LANES)
        return c

    loop(16, finish)

    def write(x, c):
        for p in range(PROBES):
            for h in range(2):
                row = h * PROBES + p
                solution_ref[p, x, pl.ds(8 * h, 8), :] = s["flip"][x, pl.ds(row, 8, stride=8), :]
        return c

    loop(16, write)


MATRICES = ("c01", "c12", "p10", "p21", "c230", "c231", "p320", "p321")


def scratch_list():
    def fields(*lead):
        return pltpu.VMEM((*lead[:-1], (lead[-1] + 3) // 4 * 4, 8, LANES), F32)

    out = {"flip": pltpu.VMEM((16, 64, LANES), F32), "lanes": pltpu.VMEM((8, LANES, LANES), jnp.bfloat16)}
    for name in ("b0", "d0", "w0"):
        out[name] = fields(16, 8)
    out["v0"] = fields(3, 18, 10)
    out["r0"] = fields(3, 2, 8)
    out["p0"] = fields(3, 2, 8)
    out["r0y"] = fields(3, 2)
    out["p0y"] = fields(3, 2)
    out["ends"] = fields(16, 1)
    out["f1"] = fields(8, 4)
    out["f2"] = fields(4, 2)
    out["f3"] = fields(2, 1)
    out["t3"] = fields(4, 2)
    for level in (1, 2):
        for name in (f"b{level}", f"w{level}", f"v{level}a", f"v{level}b"):
            out[name] = fields(*HELD[level])
        out[f"d{level}"] = fields(*CORE[level])
    out["e1"] = fields(8, 4)
    out["t1"] = fields(8, 4)
    out["e2"] = fields(6, 4)
    out["t2"] = fields(6, 4)
    out["e3"] = fields(6, 5)
    out["m1"] = fields(3, 3, 3, 4, 4)
    out["y1"] = fields(3, 3, 3, 2)
    out["y1out"] = fields(3, 2)
    out["m2"] = fields(3, 3, 3, 3, 2)
    out["z"] = fields(2, 16, 8)
    out["q"] = fields(2, 16, 8)
    out["g3"] = fields(3, 8, 4)
    out["a1"] = fields(2, 8, 4)
    out["a2"] = fields(2, 4)
    out["gw"] = fields(8, 4)
    out["gv"] = fields(2, 10, 6)
    out["count"] = fields(72)
    out["send"] = pltpu.SemaphoreType.DMA((3,))
    out["recv"] = pltpu.SemaphoreType.DMA((3,))
    out["xsend"] = pltpu.SemaphoreType.DMA((2, 3))
    out["xrecv"] = pltpu.SemaphoreType.DMA((2, 3))
    out["gsend"] = pltpu.SemaphoreType.DMA((7,))
    out["grecv"] = pltpu.SemaphoreType.DMA((7,))
    return out


def solution(mesh):
    counts = {a: mesh.shape[a] for a in ("gx", "gy", "gz")}

    def step(kappa_sq, probe_bits):
        cells = probe_bits[0].size * counts["gx"] * counts["gy"] * counts["gz"]
        whole, norms = pl.pallas_call(
            functools.partial(kernel_body, counts, cells),
            out_shape=(
                jax.ShapeDtypeStruct(probe_bits.shape, F32),
                jax.ShapeDtypeStruct((8, LANES), F32),
            ),
            in_specs=[pl.BlockSpec(memory_space=pltpu.VMEM)] * 2,
            out_specs=(pl.BlockSpec(memory_space=pltpu.VMEM),) * 2,
            scratch_shapes=list(scratch_list().values()),
            compiler_params=pltpu.CompilerParams(
                collective_id=0, has_side_effects=True, vmem_limit_bytes=40 * 2**20
            ),
            name="solve",
        )(kappa_sq, probe_bits)
        return whole, norms[:PROBES, 0]

    return jax.shard_map(
        step,
        mesh=mesh,
        in_specs=(P("gx", "gz", "gy"), P(None, "gx", "gz", "gy")),
        out_specs=(P(None, "gx", "gz", "gy"), P()),
        check_vma=False,
    )
```

time: 131 us -> 98.3 us (0.75)
  Pallas kernels: 127 us -> 94.1 us
    pallas_call x1, Pallas kernels: 127 us -> 94.1 us  [step(): pl.pallas_call(functools.partial(kernel_body, counts, cells), out_shape=(...]
where the time goes in v3:
time: 98.3 us; the launch traced here: 98.1 us
  Pallas kernels  94.1 us (96%)
  local copies, waits for them, and re-layouts  3.36 us (3%)
    pallas_call x1, Pallas kernels, step(): pl.pallas_call(functools.partial(kernel_body, counts, cells), out_shape=(...  94.1 us
    unnamed x5, local copies, waits for them, and re-layouts  2.73 us

profile of v3, /device:TPU:0, one launch (start us, length us, event | category | flops | bytes accessed | tf_op | source)
XLA Modules:
  0.0 98.1 jit_solution(3801053969709052755)
XLA Ops:
  0.6 0.0 copy-start
  0.6 1.0 %copy-done = s32[4,16,16,128]{3,2,1,0:T(8,128)S(1)} copy-done((s32[4,16,16,128]{3,2,1,0:T(8,128)S(1)}, s32[4,16,16,128]{3,2,1,0:T(8,128)}, u32[]{:S(2)}) %copy-start) | copy-done | bytes 524312
  1.7 0.0 copy-start.1
  1.7 0.9 copy-done.1
  2.6 94.1 %solve.1 = (f32[4,16,16,128]{3,2,1,0:T(8,128)S(1)}, f32[8,128]{1,0:T(8,128)S(1)}) custom-call(f32[16,16,128]{2,1,0:T(8,128)S(1)} %copy-done.1, s32[4,16,16,128]{3,2,1,0:T(8,128)S(1)} %copy-done), custom_call_target="tpu_custom_call" | custom-call | tf_op jit(solution)/shard_map/solve/pallas_call | solution.py:803
  96.7 0.6 slice_reduce_fusion
  97.3 0.8 copy.5
Async XLA Ops:
  0.6 1.0 %copy-start = (s32[4,16,16,128]{3,2,1,0:T(8,128)S(1)}, s32[4,16,16,128]{3,2,1,0:T(8,128)}, u32[]{:S(2)}) copy-start(s32[4,16,16,128]{3,2,1,0:T(8,128)} %bits_ref.1) | copy-start | bytes 1572868
  1.7 0.9 copy-start.1

commit v4 on v3

--- a/solution.py
+++ b/solution.py
@@ -212,22 +212,53 @@
                     here = (near["gx"] == x) & (near["gz"] == z) & (near["gy"] == y)
                     pl.when(here)(functools.partial(wait_for, count_of(x, z, y), send, recv))
 
-    def exchange(which):
+    def exchange(which, cell, meanwhile=None):
         v = s["v0"].at[which]
         got = s["r0"].at[which]
         pack = s["p0"].at[which]
         yin = s["r0y"].at[which]
         yout = s["p0y"].at[which]
         low_rows = rows_of((8, LANES)) < HALF
+        inner = pl.ds(1, 8)
+
+        def send(steps, src, dst):
+            c = pltpu.make_async_remote_copy(
+                src_ref=src,
+                dst_ref=dst,
+                send_sem=s["send"].at[which],
+                recv_sem=s["recv"].at[which],
+                device_id=device(steps),
+                device_id_type=MESH,
+            )
+            pl.when(exists(steps))(c.start)
+
+        def fill_z(x, carry):
+            v[x + 1, pl.ds(1, 1)] = cell(x, 0, 1)
+            v[x + 1, pl.ds(8, 1)] = cell(x, 7, 8)
+            return carry
+
+        loop(16, fill_z)
 
         def pack_z(x, carry):
             pack[0, x] = jnp.where(low_rows, v[x + 1, 1], swap_halves(v[x + 9, 1]))
             pack[1, x] = jnp.where(low_rows, swap_halves(v[x + 1, 8]), v[x + 9, 8])
             return carry
 
-        loop(8, pack_z, 0, 4)
+        loop(8, pack_z)
+        send((0, -1, 0), pack.at[0], got.at[1])
+        send((0, 1, 0), pack.at[1], got.at[0])
+        for x in (0, 15):
+            v[x + 1, pl.ds(2, 6)] = cell(x, 1, 7)
+        send((-1, 0, 0), v.at[1, inner], v.at[17, inner])
+        send((1, 0, 0), v.at[16, inner], v.at[0, inner])
 
         group = ((lane + 1) & (LANES - 1)) // 16
+
+        def fill(x, carry):
+            v[x + 2, pl.ds(2, 6)] = cell(x + 1, 1, 7)
+            return carry
+
+        loop(14, fill)
 
         def pack_y(x, carry):
             low, high = carry
@@ -240,25 +271,11 @@
             return low, high
 
         zero = jnp.zeros((8, LANES), F32)
-        yout[0], yout[1] = loop(16, pack_y, (zero, zero), 8)
-        inner = pl.ds(1, 8)
-        for steps, src, dst in (
-            ((0, -1, 0), pack.at[0], got.at[1]),
-            ((0, 1, 0), pack.at[1], got.at[0]),
-            ((-1, 0, 0), v.at[1, inner], v.at[17, inner]),
-            ((1, 0, 0), v.at[16, inner], v.at[0, inner]),
-            ((0, 0, -1), yout.at[0], yin.at[1]),
-            ((0, 0, 1), yout.at[1], yin.at[0]),
-        ):
-            c = pltpu.make_async_remote_copy(
-                src_ref=src,
-                dst_ref=dst,
-                send_sem=s["send"].at[which],
-                recv_sem=s["recv"].at[which],
-                device_id=device(steps),
-                device_id_type=MESH,
-            )
-            pl.when(exists(steps))(c.start)
+        yout[0], yout[1] = loop(16, pack_y, (zero, zero))
+        send((0, 0, -1), yout.at[0], yin.at[1])
+        send((0, 0, 1), yout.at[1], yin.at[0])
+        if meanwhile is not None:
+            meanwhile()
         wait_near(lambda x, z, y: 8 * (x + z) + y, s["send"].at[which], s["recv"].at[which])
 
         def unpack_z(x, carry):
@@ -279,31 +296,26 @@
 
         loop(16, unpack_y, 0, 8)
 
-    def neighbours(which, x):
+    def neighbours(which, x, z0=0, z1=8):
         v = s["v0"].at[which]
-        here = v[x + 1, pl.ds(1, 8)]
-        total = v[x, pl.ds(1, 8)] + v[x + 2, pl.ds(1, 8)]
-        total = total + (v[x + 1, pl.ds(0, 8)] + v[x + 1, pl.ds(2, 8)])
+        inner = pl.ds(1 + z0, z1 - z0)
+        here = v[x + 1, inner]
+        total = v[x, inner] + v[x + 2, inner]
+        total = total + (v[x + 1, pl.ds(z0, z1 - z0)] + v[x + 1, pl.ds(z0 + 2, z1 - z0)])
         ends = s["ends"][x, 0]
-        ends = jnp.stack([ends] + [turn(ends, LANES - 16 * z) for z in range(1, 8)])
-        at_lane = lanes_of((8, 8, LANES))
+        ends = jnp.stack([turn(ends, LANES - 16 * z) if z else ends for z in range(z0, z1)])
+        at_lane = lanes_of((z1 - z0, 8, LANES))
         before = jnp.where(at_lane == 0, ends, turn(here, 1))
         after = jnp.where(at_lane == LANES - 1, ends, turn(here, LANES - 1))
         return here, total + (before + after)
 
-    def put(which, row, unroll):
-        def body(x, carry):
-            s["v0"][which, x + 1, pl.ds(1, 8)] = row(x)
-            return carry
-
-        loop(16, body, 0, unroll)
-
-    def sweep(which, into):
-        def row(x):
-            here, around = neighbours(which, x)
-            return 0.2 * here + s["w0"][x] * (s["b0"][x] + around)
-
-        put(into, row, 4)
+    def swept(which):
+        def cell(x, z0, z1):
+            inner = pl.ds(z0, z1 - z0)
+            here, around = neighbours(which, x, z0, z1)
+            return 0.2 * here + s["w0"][x, inner] * (s["b0"][x, inner] + around)
+
+        return cell
 
     def start_exchange(level, n, field):
         if level == 1:
@@ -598,17 +610,7 @@
         total = folded(s["a2"][n])
         return [total[:, j : j + 1] for j in range(count)]
 
-    moved_rows(s["t1"], s["f1"], "c01", 4)
-
-    def pair_up(x, carry):
-        s["f2"][x, pl.ds(0, 2)] = pair_sum(s["f1"][pl.ds(2 * x, 2)])[0]
-        return carry
-
-    loop(4, pair_up)
     pl.semaphore_wait(barrier, greeted)
-    start_exchange(1, 0, s["f1"])
-    s["t3"][:, pl.ds(0, 2)] = moved(s["f2"][:, pl.ds(0, 2)], "c12")
-    start_exchange(2, 0, s["t3"])
 
     def coefficients_held():
         finish_exchange(1, 0, s["v1a"])
@@ -652,39 +654,65 @@
         held_up(1, s["t2"], lambda i: (i - 1) // 2, s["e1"], 3)
         moved_rows(s["e1"], s["t1"], "p10", 4)
 
-    def corrected(x):
-        e = s["t1"][x // 2]
-        return s["v0"][1, x + 1, pl.ds(1, 8)] + jnp.stack([e, e], axis=1).reshape(8, 8, LANES)
+    def begun(x, z0, z1):
+        inner = pl.ds(z0, z1 - z0)
+        return s["w0"][x, inner] * s["b0"][x, inner]
+
+    def corrected(x, z0, z1):
+        e = s["t1"].at[x // 2]
+        e = jnp.stack([e[z // 2] for z in range(z0, z1)])
+        return s["v0"][1, x + 1, pl.ds(1 + z0, z1 - z0)] + e
+
+    def coarse_kappa():
+        moved_rows(s["t1"], s["f1"], "c01", 4)
+
+        def pair_up(x, carry):
+            s["f2"][x, pl.ds(0, 2)] = pair_sum(s["f1"][pl.ds(2 * x, 2)])[0]
+            return carry
+
+        loop(4, pair_up)
+        start_exchange(1, 0, s["f1"])
+        s["t3"][:, pl.ds(0, 2)] = moved(s["f2"][:, pl.ds(0, 2)], "c12")
+        start_exchange(2, 0, s["t3"])
+
+    def first_sums():
+        def body(x, c):
+            z = s["z"][0, x]
+            b = s["flip"][x].reshape(8, 8, LANES)
+            return c[0] + folded(b * z), c[1] + folded(z * s["q"][0, x])
+
+        sum_start(loop(16, body, (jnp.zeros((8, LANES), F32),) * 2), 0)
 
     def cycle(n, carry):
-        put(0, lambda x: s["w0"][x] * s["b0"][x], 2)
-        exchange(0)
-        sweep(0, 1)
-        exchange(1)
+        def meanwhile():
+            pl.when(n == 1)(coarse_kappa)
+            pl.when(n == 2)(first_sums)
+
+        exchange(0, begun, meanwhile)
+        exchange(1, swept(0))
         below(n)
-        put(0, corrected, 2)
-        exchange(0)
-        sweep(0, 1)
-        exchange(1)
-        sweep(1, 2)
-        exchange(2)
+        exchange(0, corrected)
+        exchange(1, swept(0))
+        exchange(2, swept(1))
 
         def apply(x, c):
             here, around = neighbours(2, x)
             q = s["d0"][x] * here - around
             s["z"][n - 1, x] = here
             s["q"][n - 1, x] = q
-            b = s["b0"][x]
-
-            @pl.when(n == 1)
-            def _():
-                s["flip"][x] = b.reshape(64, LANES)
-                s["b0"][x] = q
-
-            return c[0] + folded(b * here), c[1] + folded(here * q)
-
-        dots = loop(16, apply, (jnp.zeros((8, LANES), F32),) * 2, 2)
-        pl.when(n == 1)(lambda: sum_start(dots, 0))
+            return c
+
+        loop(16, apply)
+
+        @pl.when(n == 1)
+        def _():
+            def shift(x, c):
+                s["flip"][x] = s["b0"][x].reshape(64, LANES)
+                s["b0"][x] = s["q"][0, x]
+                return c
+
+            loop(16, shift)
+
         return carry
 
     lax.fori_loop(1, 3, cycle, 0)

time: 98.3 us -> 92.7 us (0.943)
  Pallas kernels: 94.1 us -> 88.6 us
    pallas_call x1, Pallas kernels: 94.1 us -> 88.6 us  [step(): pl.pallas_call(functools.partial(kernel_body, counts, cells), out_shape=(...]
where the time goes in v4:
time: 92.7 us; the launch traced here: 92.6 us
  Pallas kernels  88.6 us (96%)
  local copies, waits for them, and re-layouts  3.36 us (4%)
    pallas_call x1, Pallas kernels, step(): pl.pallas_call(functools.partial(kernel_body, counts, cells), out_shape=(...  88.6 us
    unnamed x5, local copies, waits for them, and re-layouts  2.73 us

profile of v4, /device:TPU:0, one launch (start us, length us, event | category | flops | bytes accessed | tf_op | source)
XLA Modules:
  0.0 92.6 jit_solution(13583183136893676387)
XLA Ops:
  0.6 0.0 copy-start
  0.6 1.0 %copy-done = s32[4,16,16,128]{3,2,1,0:T(8,128)S(1)} copy-done((s32[4,16,16,128]{3,2,1,0:T(8,128)S(1)}, s32[4,16,16,128]{3,2,1,0:T(8,128)}, u32[]{:S(2)}) %copy-start) | copy-done | bytes 524312
  1.7 0.0 copy-start.1
  1.7 0.9 copy-done.1
  2.6 88.6 %solve.1 = (f32[4,16,16,128]{3,2,1,0:T(8,128)S(1)}, f32[8,128]{1,0:T(8,128)S(1)}) custom-call(f32[16,16,128]{2,1,0:T(8,128)S(1)} %copy-done.1, s32[4,16,16,128]{3,2,1,0:T(8,128)S(1)} %copy-done), custom_call_target="tpu_custom_call" | custom-call | tf_op jit(solution)/shard_map/solve/pallas_call | solution.py:831
  91.2 0.6 slice_reduce_fusion
  91.8 0.8 copy.5
Async XLA Ops:
  0.6 1.0 %copy-start = (s32[4,16,16,128]{3,2,1,0:T(8,128)S(1)}, s32[4,16,16,128]{3,2,1,0:T(8,128)}, u32[]{:S(2)}) copy-start(s32[4,16,16,128]{3,2,1,0:T(8,128)} %bits_ref.1) | copy-start | bytes 1572868
  1.7 0.9 copy-start.1

commit v5 on v4

--- a/solution.py
+++ b/solution.py
@@ -58,9 +58,16 @@
     def device(steps):
         return {a: me[a] + d for a, d in zip(axes, steps)}
 
-    around_me = [
-        (i, j, k) for i in (-1, 0, 1) for j in (-1, 0, 1) for k in (-1, 0, 1) if (i, j, k) != (0, 0, 0)
-    ]
+    around_me = sorted(
+        (
+            (i, j, k)
+            for i in (-1, 0, 1)
+            for j in (-1, 0, 1)
+            for k in (-1, 0, 1)
+            if (i, j, k) != (0, 0, 0)
+        ),
+        key=lambda steps: -sum(d * d for d in steps),
+    )
 
     def clear_faces(i, carry):
         for x in (0, 17):
@@ -70,11 +77,11 @@
         return carry
 
     loop(3, clear_faces)
-    for name in ("m1", "y1", "m2"):
+    for name in ("m1", "z1", "y1", "m2"):
         ref = s[name]
 
         def clear(i, carry, ref=ref):
-            for j in range(3):
+            for j in range(ref.shape[2]):
                 ref[i // 3, lax.rem(i, 3), j] = jnp.zeros(ref.shape[3:], F32)
             return carry
 
@@ -325,6 +332,16 @@
                 return carry
 
             loop(4, pack_x, 0, 2)
+
+            low_rows = rows_of((3, 8, LANES)) < HALF
+            for i in range(2):
+                one, two = (s["m1"].at[n, 1, 1, i + 2 * k] for k in range(2))
+                s["z1out"][n, 0, i, pl.ds(0, 3)] = jnp.where(
+                    low_rows, one[pl.ds(0, 3)], swap_halves(two[pl.ds(0, 3)])
+                )
+                s["z1out"][n, 1, i, pl.ds(0, 3)] = jnp.where(
+                    low_rows, swap_halves(one[pl.ds(1, 3)]), two[pl.ds(1, 3)]
+                )
 
             def pack_y(x, carry):
                 low, high = carry
@@ -357,13 +374,17 @@
                 dst = s["y1"].at[n, 1 - i, 1 - j, side]
             else:
                 if j == 0:
-                    part = (pl.ds(0 if i < 0 else 2, 2),)
-                elif i == 0:
-                    part = (slice(None), pl.ds(0 if j < 0 else 1, 3))
+                    part = pl.ds(0 if i < 0 else 2, 2)
+                    src = s["m1"].at[n, 1, 1, part]
+                    dst = s["m1"].at[n, 1 - i, 1 - j, part]
                 else:
-                    part = (pl.ds(0 if i < 0 else 3, 1), pl.ds(0 if j < 0 else 2, 2))
-                src = s["m1"].at[(n, 1, 1, *part)]
-                dst = s["m1"].at[(n, 1 - i, 1 - j, *part)]
+                    side = 0 if j < 0 else 1
+                    if i == 0:
+                        part = (slice(None), pl.ds(0, 3))
+                    else:
+                        part = (pl.ds(0 if i < 0 else 1, 1), pl.ds(0 if j < 0 else 1, 2))
+                    src = s["z1out"].at[(n, side, *part)]
+                    dst = s["z1"].at[(n, 1 - i, 1 - side, *part)]
             c = pltpu.make_async_remote_copy(
                 src_ref=src,
                 dst_ref=dst,
@@ -378,7 +399,7 @@
         def count_of(x, z, y):
             if level == 2:
                 return 2 * ((x + 1) * (z + 1) * (y + 1) - 1)
-            return 8 * x + 12 * z + 2 * x * z + (x + 1) * (z + 1) * y
+            return 8 * x + 6 * z + 2 * x * z + (x + 1) * (z + 1) * y
 
         wait_near(count_of, s["xsend"].at[level - 1, n], s["xrecv"].at[level - 1, n])
         low_rows = rows_of((8, LANES)) < HALF
@@ -391,9 +412,14 @@
 
             def source(j, z):
                 if level == 1:
-                    mid = turn(
-                        s["m1"][n, far, j, at_x // 2, z], 32 + 64 * lax.rem(at_x, 2)
-                    )
+                    pair = at_x // 2
+                    if j == 1:
+                        mid = s["m1"][n, far, 1, pair, z]
+                    else:
+                        mid = s["z1"][n, far, j // 2, lax.rem(pair, 2), z - 1 if j == 0 else z]
+                        there = (pair < 2) if j == 0 else (pair >= 2)
+                        mid = jnp.where(there, swap_halves(mid), mid)
+                    mid = turn(mid, 32 + 64 * lax.rem(at_x, 2))
                     at = 4 * (4 * at_x + z)
                     left = turn(s["y1"][n, far, j, 0], lax.rem(28 - at + 2 * LANES, LANES))
                     right = turn(s["y1"][n, far, j, 1], lax.rem(96 - at + 2 * LANES, LANES))
@@ -803,6 +829,8 @@
     out["t2"] = fields(6, 4)
     out["e3"] = fields(6, 5)
     out["m1"] = fields(3, 3, 3, 4, 4)
+    out["z1"] = fields(3, 3, 2, 2, 3)
+    out["z1out"] = fields(3, 2, 2, 3)
     out["y1"] = fields(3, 3, 3, 2)
     out["y1out"] = fields(3, 2)
     out["m2"] = fields(3, 3, 3, 3, 2)

time: 92.7 us -> 90.9 us (0.981)
  Pallas kernels: 88.6 us -> 86.7 us
    pallas_call x1, Pallas kernels: 88.6 us -> 86.7 us  [step(): pl.pallas_call(functools.partial(kernel_body, counts, cells), out_shape=(...]
where the time goes in v5:
time: 90.9 us; the launch traced here: 90.7 us
  Pallas kernels  86.7 us (95%)
  local copies, waits for them, and re-layouts  3.36 us (4%)
    pallas_call x1, Pallas kernels, step(): pl.pallas_call(functools.partial(kernel_body, counts, cells), out_shape=(...  86.7 us
    unnamed x5, local copies, waits for them, and re-layouts  2.73 us

profile of v5, /device:TPU:0, one launch (start us, length us, event | category | flops | bytes accessed | tf_op | source)
XLA Modules:
  0.0 90.7 jit_solution(12270905427028319928)
XLA Ops:
  0.6 0.0 copy-start
  0.6 1.0 %copy-done = s32[4,16,16,128]{3,2,1,0:T(8,128)S(1)} copy-done((s32[4,16,16,128]{3,2,1,0:T(8,128)S(1)}, s32[4,16,16,128]{3,2,1,0:T(8,128)}, u32[]{:S(2)}) %copy-start) | copy-done | bytes 524312
  1.7 0.0 copy-start.1
  1.7 0.9 copy-done.1
  2.6 86.7 %solve.1 = (f32[4,16,16,128]{3,2,1,0:T(8,128)S(1)}, f32[8,128]{1,0:T(8,128)S(1)}) custom-call(f32[16,16,128]{2,1,0:T(8,128)S(1)} %copy-done.1, s32[4,16,16,128]{3,2,1,0:T(8,128)S(1)} %copy-done), custom_call_target="tpu_custom_call" | custom-call | tf_op jit(solution)/shard_map/solve/pallas_call | solution.py:859
  89.3 0.6 slice_reduce_fusion
  89.9 0.8 copy.5
Async XLA Ops:
  0.6 1.0 %copy-start = (s32[4,16,16,128]{3,2,1,0:T(8,128)S(1)}, s32[4,16,16,128]{3,2,1,0:T(8,128)}, u32[]{:S(2)}) copy-start(s32[4,16,16,128]{3,2,1,0:T(8,128)} %bits_ref.1) | copy-start | bytes 1572868
  1.7 0.9 copy-start.1

commit v6 on v5

--- a/solution.py
+++ b/solution.py
@@ -495,7 +495,7 @@
             return carry
 
         loop(xs, begin)
-        held_sweep(level, s[f"v{level}a"], s[f"v{level}b"], 1)
+        held_sweep(level, s[f"v{level}a"], s[f"v{level}b"], reach - 1)
         z0, z1 = reach, zs - reach
         inner = pl.ds(z0, z1 - z0)
 
@@ -511,6 +511,9 @@
             return carry
 
         loop((xs - 2 * reach) // 2, body, 0, 2)
+
+    def held_rest(level):
+        held_sweep(level, s[f"v{level}a"], s[f"v{level}b"], 1)
 
     def held_up(level, coarse, spread, out, last_margin):
         xs, zs = HELD[level]
@@ -669,10 +672,12 @@
         held_down(1)
         s["t3"][:, pl.ds(0, 2)] = moved(s["f2"][:, pl.ds(0, 2)], "c12")
         start_exchange(2, n, s["t3"])
+        held_rest(1)
         finish_exchange(2, n, s["b2"])
         held_down(2)
+        gather_start(n)
+        held_rest(2)
         pl.when(n == 1)(coarse_coefficients)
-        gather_start(n)
         gather_finish(n)
         coarsest(n)
         held_up(2, s["e3"], lambda i: i // 2, s["e2"], 3)

time: 90.9 us -> 90.3 us (level)
  no operation moved by 1% of the time
where the time goes in v6:
time: 90.3 us; the launch traced here: 90.1 us
  Pallas kernels  86.1 us (95%)
  local copies, waits for them, and re-layouts  3.36 us (4%)
    pallas_call x1, Pallas kernels, step(): pl.pallas_call(functools.partial(kernel_body, counts, cells), out_shape=(...  86.1 us
    unnamed x5, local copies, waits for them, and re-layouts  2.73 us

profile of v6, /device:TPU:0, one launch (start us, length us, event | category | flops | bytes accessed | tf_op | source)
XLA Modules:
  0.0 90.1 jit_solution(1364714097969699256)
XLA Ops:
  0.6 0.0 copy-start
  0.6 1.0 %copy-done = s32[4,16,16,128]{3,2,1,0:T(8,128)S(1)} copy-done((s32[4,16,16,128]{3,2,1,0:T(8,128)S(1)}, s32[4,16,16,128]{3,2,1,0:T(8,128)}, u32[]{:S(2)}) %copy-start) | copy-done | bytes 524312
  1.7 0.0 copy-start.1
  1.7 0.9 %copy-done.1 = f32[16,16,128]{2,1,0:T(8,128)S(1)} copy-done((f32[16,16,128]{2,1,0:T(8,128)S(1)}, f32[16,16,128]{2,1,0:T(8,128)}, u32[]{:S(2)}) %copy-start.1) | copy-done | bytes 131096
  2.6 86.1 %solve.1 = (f32[4,16,16,128]{3,2,1,0:T(8,128)S(1)}, f32[8,128]{1,0:T(8,128)S(1)}) custom-call(f32[16,16,128]{2,1,0:T(8,128)S(1)} %copy-done.1, s32[4,16,16,128]{3,2,1,0:T(8,128)S(1)} %copy-done), custom_call_target="tpu_custom_call" | custom-call | tf_op jit(solution)/shard_map/solve/pallas_call | solution.py:864
  88.7 0.6 slice_reduce_fusion
  89.3 0.8 copy.5
Async XLA Ops:
  0.6 1.0 %copy-start = (s32[4,16,16,128]{3,2,1,0:T(8,128)S(1)}, s32[4,16,16,128]{3,2,1,0:T(8,128)}, u32[]{:S(2)}) copy-start(s32[4,16,16,128]{3,2,1,0:T(8,128)} %bits_ref.1) | copy-start | bytes 1572868
  1.7 0.9 %copy-start.1 = (f32[16,16,128]{2,1,0:T(8,128)S(1)}, f32[16,16,128]{2,1,0:T(8,128)}, u32[]{:S(2)}) copy-start(f32[16,16,128]{2,1,0:T(8,128)} %kappa_ref.1) | copy-start | bytes 393220

commit v7 on v6

--- a/solution.py
+++ b/solution.py
@@ -706,11 +706,20 @@
         s["t3"][:, pl.ds(0, 2)] = moved(s["f2"][:, pl.ds(0, 2)], "c12")
         start_exchange(2, 0, s["t3"])
 
+        def keep_b(x, carry):
+            s["flip"][x] = s["b0"][x].reshape(64, LANES)
+            return carry
+
+        loop(16, keep_b)
+
     def first_sums():
         def body(x, c):
-            z = s["z"][0, x]
+            z = s["z"][1, x]
+            q = s["q"][1, x]
+            s["z"][0, x] = z
+            s["q"][0, x] = q
             b = s["flip"][x].reshape(8, 8, LANES)
-            return c[0] + folded(b * z), c[1] + folded(z * s["q"][0, x])
+            return c[0] + folded(b * z), c[1] + folded(z * q)
 
         sum_start(loop(16, body, (jnp.zeros((8, LANES), F32),) * 2), 0)
 
@@ -729,8 +738,8 @@
         def apply(x, c):
             here, around = neighbours(2, x)
             q = s["d0"][x] * here - around
-            s["z"][n - 1, x] = here
-            s["q"][n - 1, x] = q
+            s["z"][1, x] = here
+            s["q"][1, x] = q
             return c
 
         loop(16, apply)
@@ -738,8 +747,7 @@
         @pl.when(n == 1)
         def _():
             def shift(x, c):
-                s["flip"][x] = s["b0"][x].reshape(64, LANES)
-                s["b0"][x] = s["q"][0, x]
+                s["b0"][x] = s["q"][1, x]
                 return c
 
             loop(16, shift)

time: 90.3 us -> 90.2 us (level)
  no operation moved by 1% of the time
where the time goes in v7:
time: 90.2 us; the launch traced here: 90.1 us
  Pallas kernels  86.1 us (95%)
  local copies, waits for them, and re-layouts  3.36 us (4%)
    pallas_call x1, Pallas kernels, step(): pl.pallas_call(functools.partial(kernel_body, counts, cells), out_shape=(...  86.1 us
    unnamed x5, local copies, waits for them, and re-layouts  2.73 us

profile of v7, /device:TPU:0, one launch (start us, length us, event | category | flops | bytes accessed | tf_op | source)
XLA Modules:
  0.0 90.1 jit_solution(6723350599867738563)
XLA Ops:
  0.6 0.0 copy-start
  0.6 1.0 %copy-done = s32[4,16,16,128]{3,2,1,0:T(8,128)S(1)} copy-done((s32[4,16,16,128]{3,2,1,0:T(8,128)S(1)}, s32[4,16,16,128]{3,2,1,0:T(8,128)}, u32[]{:S(2)}) %copy-start) | copy-done | bytes 524312
  1.7 0.0 copy-start.1
  1.7 0.9 %copy-done.1 = f32[16,16,128]{2,1,0:T(8,128)S(1)} copy-done((f32[16,16,128]{2,1,0:T(8,128)S(1)}, f32[16,16,128]{2,1,0:T(8,128)}, u32[]{:S(2)}) %copy-start.1) | copy-done | bytes 131096
  2.6 86.1 %solve.1 = (f32[4,16,16,128]{3,2,1,0:T(8,128)S(1)}, f32[8,128]{1,0:T(8,128)S(1)}) custom-call(f32[16,16,128]{2,1,0:T(8,128)S(1)} %copy-done.1, s32[4,16,16,128]{3,2,1,0:T(8,128)S(1)} %copy-done), custom_call_target="tpu_custom_call" | custom-call | tf_op jit(solution)/shard_map/solve/pallas_call | solution.py:872
  88.6 0.6 slice_reduce_fusion
  89.3 0.8 copy.5
Async XLA Ops:
  0.6 1.0 %copy-start = (s32[4,16,16,128]{3,2,1,0:T(8,128)S(1)}, s32[4,16,16,128]{3,2,1,0:T(8,128)}, u32[]{:S(2)}) copy-start(s32[4,16,16,128]{3,2,1,0:T(8,128)} %bits_ref.1) | copy-start | bytes 1572868
  1.7 0.9 %copy-start.1 = (f32[16,16,128]{2,1,0:T(8,128)S(1)}, f32[16,16,128]{2,1,0:T(8,128)}, u32[]{:S(2)}) copy-start(f32[16,16,128]{2,1,0:T(8,128)} %kappa_ref.1) | copy-start | bytes 393220
